TPU v7x, 128 devices: a whole 4x4x4 slice. The times are simulated.
128 devices in a mesh: tp: 128 (over z, y, x, core).
Axes of the slice: x: 4, y: 4, z: 4, core: 2. Of those that a mesh axis runs over, the one named last changes fastest.
Arguments:
- tok_ids: int32 [2, 128], replicated
- next_ids: int32 [2, 128], replicated
- seq_lens: int32 [128], replicated
- embed: bfloat16 [256000, 2048], P('tp')
- ln_gain: bfloat16 [2048], replicated
- w_in: bfloat16 [2048, 35328], P(None, 'tp')
- w_out: bfloat16 [18432, 2048], P('tp')
- final_gain: bfloat16 [2048], replicated
- k_cache: bfloat16 [128, 1024, 256], P('tp')
- v_cache: bfloat16 [128, 1024, 256], P('tp')
Outputs:
- output 1: float32 [2, 128], replicated
- output 2: bfloat16 [128, 1024, 256], P('tp')
- output 3: bfloat16 [128, 1024, 256], P('tp')
All inputs are finite; a program needn't handle non-finite values.
Results may differ from a plain program's by a relative error of at most 0.001.
Values are sent between devices in bfloat16 or wider.
A program may use at most 1 GiB of HBM per device.

v0:
```python
import jax
import jax.numpy as jnp
from jax import lax
from jax.sharding import PartitionSpec as P

ROPE_BASE = 10000.0
NORM_EPS = 1e-6


def layer_norm(values, gain_vec):
    centered = values.astype(jnp.float32)
    centered = centered - jnp.mean(centered, axis=-1, keepdims=True)
    variance = jnp.mean(jnp.square(centered), axis=-1, keepdims=True)
    scaled = centered * lax.rsqrt(variance + NORM_EPS) * gain_vec.astype(jnp.float32)
    return scaled.astype(jnp.bfloat16)


def rotary(vectors, positions):
    half_dim = vectors.shape[-1] // 2
    inv_freq = ROPE_BASE ** (-jnp.arange(half_dim, dtype=jnp.float32) / half_dim)
    angles = positions.astype(jnp.float32)[..., None] * inv_freq
    cosine = jnp.cos(angles)
    sine_val = jnp.sin(angles)
    first_half = vectors[..., :half_dim]
    second_half = vectors[..., half_dim:]
    return jnp.concatenate([first_half * cosine - second_half * sine_val, second_half * cosine + first_half * sine_val], axis=-1)


def solution(mesh):
    group_size = mesh.shape['tp']

    def device_fn(tok_ids, next_ids, seq_lens, embed_loc, ln_gain, w_in_loc, w_out_loc, final_gain, k_loc, v_loc):
        batch_size = tok_ids.shape[1]
        batch_dev = batch_size // group_size
        model_dim = embed_loc.shape[1]
        vocab_dev = embed_loc.shape[0]
        cache_len = k_loc.shape[1]
        head_dim = k_loc.shape[2]
        in_dev = w_in_loc.shape[1]
        out_dev = w_out_loc.shape[0]
        kv_dev = 2 * head_dim // group_size
        attn_dev = 2 * out_dev - in_dev + kv_dev
        ff_dev = out_dev - attn_dev
        qkv_dev = attn_dev + kv_dev
        attn_width = attn_dev * group_size
        num_heads = attn_width // head_dim
        dev_index = lax.axis_index('tp')
        vocab_start = dev_index * vocab_dev
        own_lens = lax.dynamic_slice_in_dim(seq_lens, dev_index * batch_dev, batch_dev)
        time_ids = jnp.arange(cache_len)
        step_logp = []
        for step_idx in range(tok_ids.shape[0]):
            local_ids = tok_ids[step_idx] - vocab_start
            tok_here = (local_ids >= 0) & (local_ids < vocab_dev)
            emb_rows = jnp.take(embed_loc, jnp.clip(local_ids, 0, vocab_dev - 1), axis=0)
            x_rows = lax.psum(jnp.where(tok_here[:, None], emb_rows, jnp.zeros_like(emb_rows)), 'tp')
            normed = layer_norm(x_rows, ln_gain)
            proj_out = jnp.dot(normed, w_in_loc, preferred_element_type=jnp.float32).astype(jnp.bfloat16)
            gate_proj = proj_out[:, qkv_dev:qkv_dev + ff_dev].astype(jnp.float32)
            up_proj = proj_out[:, qkv_dev + ff_dev:].astype(jnp.float32)
            mlp_act = (jax.nn.silu(gate_proj) * up_proj).astype(jnp.bfloat16)
            qkv_own = lax.all_to_all(proj_out[:, :qkv_dev], 'tp', 0, 1, tiled=True)
            positions = own_lens + step_idx
            queries = qkv_own[:, :attn_width].reshape(batch_dev, num_heads, head_dim).astype(jnp.float32)
            q_rot = (rotary(queries, positions[:, None]) * head_dim ** -0.5).astype(jnp.bfloat16)
            k_new = rotary(qkv_own[:, attn_width:attn_width + head_dim].astype(jnp.float32), positions).astype(jnp.bfloat16)
            v_new = qkv_own[:, attn_width + head_dim:]
            write_mask = time_ids[None, :, None] == positions[:, None, None]
            k_loc = jnp.where(write_mask, k_new[:, None, :], k_loc)
            v_loc = jnp.where(write_mask, v_new[:, None, :], v_loc)
            scores = jnp.einsum('bhd,btd->bht', q_rot, k_loc, preferred_element_type=jnp.float32)
            visible = time_ids[None, None, :] <= positions[:, None, None]
            attn_probs = jax.nn.softmax(jnp.where(visible, scores, -jnp.inf), axis=-1).astype(jnp.bfloat16)
            attn_out = jnp.einsum('bht,btd->bhd', attn_probs, v_loc, preferred_element_type=jnp.float32).astype(jnp.bfloat16)
            attn_cols = lax.all_to_all(attn_out.reshape(batch_dev, attn_width), 'tp', 1, 0, tiled=True)
            combined = jnp.concatenate([attn_cols, mlp_act], axis=1)
            part_out = jnp.dot(combined, w_out_loc, preferred_element_type=jnp.float32).astype(jnp.bfloat16)
            layer_out = lax.psum(part_out, 'tp')
            resid_sum = x_rows.astype(jnp.float32) + layer_out.astype(jnp.float32)
            final_normed = layer_norm(resid_sum, final_gain)
            logits = jnp.einsum('bd,vd->bv', final_normed, embed_loc, preferred_element_type=jnp.float32) * model_dim ** -0.5
            row_max = lax.pmax(jnp.max(logits, axis=1), 'tp')
            exp_sum = lax.psum(jnp.sum(jnp.exp(logits - row_max[:, None]), axis=1), 'tp')
            local_next = next_ids[step_idx] - vocab_start
            next_here = (local_next >= 0) & (local_next < vocab_dev)
            picked = jnp.take_along_axis(logits, jnp.clip(local_next, 0, vocab_dev - 1)[:, None], axis=1)[:, 0]
            target = lax.psum(jnp.where(next_here, picked, 0.0), 'tp')
            step_logp.append(target - row_max - jnp.log(exp_sum))
        return jnp.stack(step_logp), k_loc, v_loc

    cache_spec = P('tp', None, None)
    return jax.shard_map(device_fn, mesh=mesh, in_specs=(P(), P(), P(), P('tp', None), P(), P(None, 'tp'), P('tp', None), P(), cache_spec, cache_spec), out_specs=(P(), cache_spec, cache_spec), check_vma=False)
```

profile of v0, /device:TPU:1, one launch (start us, length us, event | category | flops | bytes accessed | tf_op | source)
XLA Modules:
  0.0 550.7 jit_solution(14586303352764906258)
XLA Ops:
  7.3 0.8 compare_and_fusion.1
  8.1 0.8 and_bitcast_fusion.1
  8.8 5.8 %gather_fusion = bf16[128,2048]{1,0:T(8,128)(2,1)S(1)} fusion(bf16[2000,2048]{1,0:T(8,128)(2,1)} %param.17, s32[1024]{0:T(1024)S(1)} %pad_clamp_fusion.1), kind=kCustom, calls=%fused_computation.clone | custom fusion | bytes 1049088 | tf_op jit(solution)/shard_map/jit(_take)/gather | solution.py:55
  14.7 5.9 %gather_fusion.2 = bf16[128,2048]{1,0:T(8,128)(2,1)S(1)} fusion(bf16[2000,2048]{1,0:T(8,128)(2,1)} %param.17, s32[1024]{0:T(1024)S(1)} %pad_clamp_fusion), kind=kCustom, calls=%fused_computation.2.clone | custom fusion | bytes 1049088 | tf_op jit(solution)/shard_map/jit(_take)/gather | solution.py:55
  20.6 1.2 select_select_fusion
  21.8 0.6 dynamic_slice.3
  23.7 0.6 multiply_sine_fusion.3
  24.4 0.6 multiply_sine_fusion.1
  25.0 1.2 iota_compare_fusion.2
  26.8 148.3 %all-reduce.9.cloned.1.call-done = (bf16[128,2048]{1,0:T(8,128)(2,1)}, bf16[128,2048]{1,0:T(8,128)(2,1)}) async-done(((bf16[128,2048]{1,0:T(8,128)(2,1)}, bf16[128,2048]{1,0:T(8,128)(2,1)}), (bf16[128,2048]{1,0:T(8,128)(2,1)}, bf16[128,2048]{1,0:T(8,128)(2,1)})) %all-reduce.9.cloned.1.call-update) | async-done | bytes 1048592 | tf_op jit(solution)/shard_map/psum | solution.py:56
  175.1 1.3 convert_reduce_fusion.1
  176.4 1.3 fusion.7
  177.8 1.6 convolution_convert_fusion.3
  179.5 0.8 copy.17
  180.2 6.6 %all-to-all-start = ((bf16[128,1,20]{2,1,0:T(2,128)(2,1)}), bf16[128,1,20]{2,1,0:T(2,128)(2,1)S(1)}, u32[]{:S(2)}, u32[]{:S(2)}) async-start(bf16[128,1,20]{2,1,0:T(2,128)(2,1)} %copy.17), calls=%async_computation | async-start | bytes 131072 | tf_op jit(solution)/shard_map/all_to_all | solution.py:62
  186.8 1.2 convert_reduce_fusion
  188.0 1.3 fusion.4
  189.4 1.6 convolution_convert_fusion.2
  191.1 0.8 copy.20
  191.8 4.8 all-to-all-done
  196.7 4.9 all-to-all-start.2
  202.0 9.5 %all-to-all-done.2 = bf16[128,1,20]{2,1,0:T(2,128)(2,1)S(1)} async-done(((bf16[128,1,20]{2,1,0:T(2,128)(2,1)}), bf16[128,1,20]{2,1,0:T(2,128)(2,1)S(1)}, u32[]{:S(2)}, u32[]{:S(2)}) %all-to-all-start.2) | async-done | bytes 5152 | tf_op jit(solution)/shard_map/all_to_all | solution.py:62
  211.9 0.7 subtract_bitcast_fusion.1
  212.6 1.1 fusion.73
  213.9 1.4 convolution_convert_fusion.5
  215.2 0.7 all_to_all.60
  216.0 4.5 all-to-all-start.1
  220.6 2.0 broadcast_select_fusion.1
  222.6 0.7 subtract_bitcast_fusion
  224.2 0.7 all_to_all.61
  224.9 5.4 all-to-all-done.1
  230.3 4.5 all-to-all-start.3
  235.1 1.2 convolution_convert_fusion.1
  236.3 8.4 %all-to-all-done.3 = bf16[1,128,16]{2,0,1:T(2,128)(2,1)S(1)} async-done(((bf16[1,128,16]{2,0,1:T(2,128)(2,1)}), bf16[1,128,16]{2,0,1:T(2,128)(2,1)S(1)}, u32[]{:S(2)}, u32[]{:S(2)}) %all-to-all-start.3) | async-done | bytes 4128 | tf_op jit(solution)/shard_map/all_to_all | solution.py:75
  244.7 1.2 convolution_convert_fusion
  245.9 0.8 fusion.70
  246.7 145.7 %all-reduce.7.cloned.1.call-done = (bf16[128,2048]{1,0:T(8,128)(2,1)}, bf16[128,2048]{1,0:T(8,128)(2,1)}) async-done(((bf16[128,2048]{1,0:T(8,128)(2,1)}, bf16[128,2048]{1,0:T(8,128)(2,1)}), (bf16[128,2048]{1,0:T(8,128)(2,1)}, bf16[128,2048]{1,0:T(8,128)(2,1)})) %all-reduce.7.cloned.1.call-update) | async-done | bytes 1048592 | tf_op jit(solution)/shard_map/psum | solution.py:78
  392.4 1.3 fusion.11
  393.6 1.3 multiply_reduce_fusion.1
  395.0 1.3 fusion.13
  396.3 1.3 multiply_reduce_fusion
  397.6 6.1 %fusion.75 = (f32[128]{0:T(128)S(1)}, f32[128,2000]{0,1:T(8,128)S(1)}) fusion(bf16[2000,2048]{1,0:T(8,128)(2,1)} %param.17, bf16[128,2048]{1,0:T(8,128)(2,1)} %get-tuple-element.12, bf16[128,2048]{1,0:T(8,128)(2,1)S(1)} %copy-done.2, f32[2048]{0:T(1024)S(1)} %convert_element_type.166, f32[128]{0:T(128)S(1)} %add_rsqrt_fusion.2, ...), kind=kOutput, calls=%fused_computation.178 | convolution fusion | flops 1050922880 | bytes 10274304 | tf_op jit(solution)/shard_map/bd,vd->bv/dot_general | solution.py:81
  403.8 3.4 fusion.74
  407.2 63.9 %all-reduce.1 = (f32[128]{0:T(128)S(1)}, f32[128]{0:T(128)S(1)}) all-reduce(f32[128]{0:T(128)S(1)} %get-tuple-element.47, f32[128]{0:T(128)S(1)} %get-tuple-element.49), channel_id=1, replica_groups=mesh['tp'=128] {'tp'}, use_global_device_ids=true, to_apply=%region_23.26 | all-reduce | flops 256 | bytes 2048 | tf_op jit(solution)/shard_map/pmax | solution.py:82
  471.3 1.3 gather_fusion.1
  472.6 6.0 %gather_fusion.3 = f32[128]{0:T(128)S(1)} fusion(f32[128,2000]{0,1:T(8,128)} %get-tuple-element.48, s32[128]{0:T(128)S(1)} %get-tuple-element.61), kind=kCustom, calls=%fused_computation.3.clone | custom fusion | bytes 2048 | tf_op jit(solution)/shard_map/jit(take_along_axis)/gather | solution.py:86
  478.7 1.5 exponential_reduce_fusion
  480.2 63.1 %all-reduce = (f32[128]{0:T(128)S(1)}, f32[128]{0:T(128)S(1)}, f32[128]{0:T(128)S(1)}, f32[128]{0:T(128)S(1)}) all-reduce(f32[128]{0:T(128)S(1)} %exponential_reduce_fusion, f32[128]{0:T(128)S(1)} %get-tuple-element.30, f32[128]{0:T(128)S(1)} %exponential_reduce_fusion.1, ...), channel_id=1, replica_groups=mesh['tp'=128] {'tp'}, use_global_device_ids=true, to_apply=%region_25.28 | all-reduce | flops 512 | bytes 4096 | tf_op jit(solution)/shard_map/psum | solution.py:83
  (78 shorter events, 4.1 us)
Async XLA Ops:
  7.2 170.6 %copy-start = (bf16[2048,276]{0,1:T(8,128)(2,1)S(1)}, bf16[2048,276]{0,1:T(8,128)(2,1)}, u32[]{:S(2)}) copy-start(bf16[2048,276]{0,1:T(8,128)(2,1)} %param.19) | copy-start | bytes 3391492
  7.2 14.6 %copy-start.8 = (bf16[2048]{0:T(1024)(128)(2,1)S(1)}, bf16[2048]{0:T(1024)(128)(2,1)}, u32[]{:S(2)}) copy-start(bf16[2048]{0:T(1024)(128)(2,1)} %param.18) | copy-start | bytes 12292
  7.2 14.6 %copy-start.11 = (s32[128]{0:T(128)S(1)}, s32[128]{0:T(128)}, u32[]{:S(2)}) copy-start(s32[128]{0:T(128)} %param.16) | copy-start | bytes 1540
  7.2 16.5 %copy-start.9 = (bf16[2048]{0:T(1024)(128)(2,1)S(1)}, bf16[2048]{0:T(1024)(128)(2,1)}, u32[]{:S(2)}) copy-start(bf16[2048]{0:T(1024)(128)(2,1)} %param.21) | copy-start | bytes 12292
  7.2 167.9 %all-reduce.9.cloned.1.call-start = ((), (), s32[]{:S(2)}) async-start(), calls=%async_computation.5 | async-start | bytes 2097152 | tf_op jit(solution)/shard_map/psum | solution.py:56
  14.7 197.9 %copy-start.6 = (bf16[1,1024,256]{2,1,0:T(8,128)(2,1)S(1)}, bf16[1,1024,256]{2,1,0:T(8,128)(2,1)}, u32[]{:S(2)}) copy-start(bf16[1,1024,256]{2,1,0:T(8,128)(2,1)} %param.22) | copy-start | bytes 1572868
  20.6 214.5 %copy-start.4 = (bf16[144,2048]{1,0:T(8,128)(2,1)S(1)}, bf16[144,2048]{1,0:T(8,128)(2,1)}, u32[]{:S(2)}) copy-start(bf16[144,2048]{1,0:T(8,128)(2,1)} %param.20) | copy-start | bytes 1769476
  175.1 217.2 %copy-start.2 = (bf16[128,2048]{1,0:T(8,128)(2,1)S(1)}, bf16[128,2048]{1,0:T(8,128)(2,1)}, u32[]{:S(2)}) copy-start(bf16[128,2048]{1,0:T(8,128)(2,1)} %get-tuple-element.14) | copy-start | bytes 1572868
  179.4 215.6 %copy-start.1 = (bf16[128,2048]{1,0:T(8,128)(2,1)S(1)}, bf16[128,2048]{1,0:T(8,128)(2,1)}, u32[]{:S(2)}) copy-start(bf16[128,2048]{1,0:T(8,128)(2,1)} %get-tuple-element.13) | copy-start | bytes 1572868
  180.2 16.4 %all-to-all-start = ((bf16[128,1,20]{2,1,0:T(2,128)(2,1)}), bf16[128,1,20]{2,1,0:T(2,128)(2,1)S(1)}, u32[]{:S(2)}, u32[]{:S(2)}) async-start(bf16[128,1,20]{2,1,0:T(2,128)(2,1)} %copy.17), calls=%async_computation | async-start | bytes 131072 | tf_op jit(solution)/shard_map/all_to_all | solution.py:62
  196.7 14.8 %all-to-all-start.2 = ((bf16[128,1,20]{2,1,0:T(2,128)(2,1)}), bf16[128,1,20]{2,1,0:T(2,128)(2,1)S(1)}, u32[]{:S(2)}, u32[]{:S(2)}) async-start(bf16[128,1,20]{2,1,0:T(2,128)(2,1)} %copy.20), calls=%async_computation.2 | async-start | bytes 131072 | tf_op jit(solution)/shard_map/all_to_all | solution.py:62
  216.0 14.3 %all-to-all-start.1 = ((bf16[1,128,16]{2,0,1:T(2,128)(2,1)}), bf16[1,128,16]{2,0,1:T(2,128)(2,1)S(1)}, u32[]{:S(2)}, u32[]{:S(2)}) async-start(bf16[1,128,16]{2,0,1:T(2,128)(2,1)} %all_to_all.60), calls=%async_computation.1 | async-start | bytes 131072 | tf_op jit(solution)/shard_map/all_to_all | solution.py:75
  222.6 0.8 copy-start.5
  222.6 1.3 copy-start.7
  230.3 14.3 %all-to-all-start.3 = ((bf16[1,128,16]{2,0,1:T(2,128)(2,1)}), bf16[1,128,16]{2,0,1:T(2,128)(2,1)S(1)}, u32[]{:S(2)}, u32[]{:S(2)}) async-start(bf16[1,128,16]{2,0,1:T(2,128)(2,1)} %all_to_all.61), calls=%async_computation.3 | async-start | bytes 131072 | tf_op jit(solution)/shard_map/all_to_all | solution.py:75
  234.8 157.5 %all-reduce.7.cloned.1.call-start = ((), (), s32[]{:S(2)}) async-start(), calls=%async_computation.4 | async-start | bytes 2097152 | tf_op jit(solution)/shard_map/psum | solution.py:78
  397.6 6.1 %slice-start = ((s8[8192000]{0:T(1024)(128)(4,1)}), s8[4194304]{0:T(1024)(128)(4,1)S(1)}, s32[]{:S(2)}) async-start(s8[8192000]{0:T(1024)(128)(4,1)} %bitcast.102), calls=%async_computation.6 | async-start | bytes 8388608
  397.6 6.1 %copy-start.3 = (bf16[128,2048]{1,0:T(8,128)(2,1)S(1)}, bf16[128,2048]{1,0:T(8,128)(2,1)}, u32[]{:S(2)}) copy-start(bf16[128,2048]{1,0:T(8,128)(2,1)} %get-tuple-element.11) | copy-start | bytes 1572868
  397.6 6.1 %slice-start.1 = ((s8[8192000]{0:T(1024)(128)(4,1)}), s8[3997696]{0:T(1024)(128)(4,1)S(1)}, s32[]{:S(2)}) async-start(s8[8192000]{0:T(1024)(128)(4,1)} %bitcast.102), calls=%async_computation.7 | async-start | bytes 7995392
  403.7 76.4 %copy-start.10 = (s32[2,128]{1,0:T(2,128)S(1)}, s32[2,128]{1,0:T(2,128)}, u32[]{:S(2)}) copy-start(s32[2,128]{1,0:T(2,128)} %param.15) | copy-start | bytes 3076
Sparse Core Ops, SparseCore 0:
  21.9 153.1 all-reduce.8
  246.0 146.2 all-reduce.6
where the time goes:
time: 552 us; the launch traced here: 551 us
  waiting for transfers between devices  322 us (58%)
  blocking collectives  127 us (23%)
  other arithmetic  23.9 us (4%)
  local copies, waits for them, and re-layouts  23.1 us (4%)
  starting transfers between devices  20.8 us (4%)
  matrix products  18.1 us (3%)
  between operations  15.8 us (3%)
    psum x1, waiting for transfers between devices, device_fn(): lax.psum(jnp.where(tok_here[:, None], emb_rows, jnp.zeros_like(emb_rows))...  148 us
    psum x1, waiting for transfers between devices, device_fn(): layer_out = lax.psum(part_out, 'tp')  146 us
    pmax x1, blocking collectives, device_fn(): row_max = lax.pmax(jnp.max(logits, axis=1), 'tp')  63.9 us
    psum x1, blocking collectives, device_fn(): lax.psum(jnp.sum(jnp.exp(logits - row_max[:, None]), axis=1), 'tp')  63.1 us
    all_to_all x2, waiting for transfers between devices, device_fn(): qkv_own = lax.all_to_all(proj_out[:, :qkv_dev], 'tp', 0, 1, tiled=True)  14.3 us
    all_to_all x2, waiting for transfers between devices, device_fn(): lax.all_to_all(attn_out.reshape(batch_dev, attn_width), 'tp', 1, 0, tiled...  13.7 us
    gather x2, local copies, waits for them, and re-layouts, device_fn(): jnp.take(embed_loc, jnp.clip(local_ids, 0, vocab_dev - 1), axis=0)  11.7 us
    all_to_all x2, starting transfers between devices, device_fn(): qkv_own = lax.all_to_all(proj_out[:, :qkv_dev], 'tp', 0, 1, tiled=True)  11.5 us
  transfers between devices with their start and end apart: 6, of which 6 were waited for; matrix products, arithmetic and copies ran while one was open for 3% of the time, Pallas kernels for 0%

commit v1 on v0

v1 whole, which is shorter than its diff:
```python
import jax
import jax.numpy as jnp
from jax import lax
from jax.experimental import pallas as pl
from jax.experimental.pallas import tpu as pltpu
from jax.sharding import PartitionSpec as P

ROPE_BASE = 10000.0
NORM_EPS = 1e-6
F32 = jnp.float32
BF16 = jnp.bfloat16
MESH = pl.DeviceIdType.MESH

D = 2048
VDEV = 2000
VPAD = 2048
HEADS = 8
HEAD = 256
CACHE = 1024
TILES = D // 128
QKV_DEV = 20
ATT_DEV = 16
LANE = 128
WIDE = 256
ROWS = 32
SIDE = 16
LINE = 4
SUB = 8
FOLD = 512
LINE_ORDER = (2, 1, 3)


def rem(value, size):
    return lax.rem(value, jnp.int32(size))


def div(value, size):
    return lax.div(value, jnp.int32(size))


def iota(shape, dim):
    return lax.broadcasted_iota(jnp.int32, shape, dim)


def nt_dot(left, right):
    return lax.dot_general(left, right, (((1,), (1,)), ((), ())), preferred_element_type=F32)


def nn_dot(left, right):
    return lax.dot_general(left, right, (((1,), (0,)), ((), ())), preferred_element_type=F32)


def device_of(core, line, plane):
    return div(plane, LINE) * ROWS + rem(plane, LINE) * (SUB - 6 * core) + line * (2 + 6 * core) + core


def kernel(tok_ref, next_ref, lens_ref, emb_hbm, lng_ref, win_hbm, wout_hbm, fing_ref, k_hbm, v_hbm, freq_ref,
           logp_ref, kout_hbm, vout_hbm,
           emb, win, wgu, wout, kbuf, vbuf, wq, wext, sel, hot,
           send_d, own, recv_d, send_f, recv_f, acc, fold32, afold, fold16, recv_p, x_own, gains,
           ag, unf, lhs, qlhs, qmsg, recv_q, qrows, qkrow, afbuf, amsg, recv_a, alhs, mlp, lg,
           fin_s, fin_p, fin_f, fin_d,
           ld, sd_s, sd_r, sf_s, sf_r, sp_s, sp_r, ap_s, ap_r, af_s, af_r, ad_s, ad_r,
           wd_s, wd_r, wf_s, wf_r, q_s, q_r, a_s, a_r, fp_s, fp_r, ff_s, ff_r, fd_s, fd_r):
    me = lax.axis_index('tp')
    core = rem(me, 2)
    other = 1 - core
    zc, yc, xc = div(me, ROWS), rem(div(me, SUB), LINE), rem(div(me, 2), LINE)
    line = xc * other + yc * core
    line_o = yc * other + xc * core
    plane = zc * LINE + yc * other + xc * core
    partner = me + 1 - 2 * core
    me_slot = rem(me, ROWS)
    partner_slot = rem(partner, ROWS)

    def line_dev(k):
        return device_of(core, rem(line + k, LINE), plane)

    def plane_dev(pp):
        return device_of(core, line, pp)

    def rcopy(src, dst, ss, rs, dev):
        return pltpu.make_async_remote_copy(src_ref=src, dst_ref=dst, send_sem=ss, recv_sem=rs, device_id=(dev,), device_id_type=MESH)

    def local_copies():
        out = []
        for n in range(SUB):
            cols = pl.ds(n * WIDE, WIDE)
            out.append(pltpu.make_async_copy(emb_hbm.at[:, cols], emb.at[pl.ds(0, VDEV), cols], ld.at[n]))
        out.append(pltpu.make_async_copy(win_hbm, win, ld.at[SUB]))
        out.append(pltpu.make_async_copy(wout_hbm, wout, ld.at[9]))
        out.append(pltpu.make_async_copy(k_hbm.at[0], kbuf, ld.at[10]))
        out.append(pltpu.make_async_copy(v_hbm.at[0], vbuf, ld.at[11]))
        return out

    loads = local_copies()
    for copy in loads:
        copy.start()

    wext[...] = jnp.zeros_like(wext)

    barrier = pltpu.get_barrier_semaphore()
    pl.semaphore_signal(barrier, inc=1, device_id=(partner,), device_id_type=MESH)
    for k in range(1, LINE):
        pl.semaphore_signal(barrier, inc=1, device_id=(line_dev(k),), device_id_type=MESH)

    def greet(k, carry):
        pl.semaphore_signal(barrier, inc=1, device_id=(plane_dev(rem(plane + k, SIDE)),), device_id_type=MESH)
        return carry

    lax.fori_loop(1, SIDE, greet, 0)

    emb[pl.ds(VDEV, VPAD - VDEV), :] = jnp.zeros((VPAD - VDEV, D), BF16)
    for t in range(TILES):
        gains[pl.ds(t, 1), :] = lng_ref[:, t * LANE:(t + 1) * LANE].astype(F32)
        gains[pl.ds(TILES + t, 1), :] = fing_ref[:, t * LANE:(t + 1) * LANE].astype(F32)

    row = iota((WIDE, LANE), 0)
    lane = iota((WIDE, LANE), 1)
    half = row >> 7
    row_core = core + (1 - half) * (1 - 2 * core)
    row_p = (row >> 1) & 15
    row_b = (row_p >> 2) * ROWS + (row_p & 3) * (SUB - 6 * row_core) + ((row >> 5) & 3) * (2 + 6 * row_core) + row_core
    tok_val = jnp.where((row & 1) == 0, tok_ref[0:1, :], tok_ref[1:2, :]).astype(F32)
    tok_col = jnp.sum(jnp.where(lane == row_b, tok_val, 0.0), axis=1, keepdims=True)
    local_col = tok_col.astype(jnp.int32) - me * VDEV
    for t in range(VPAD // LANE):
        hot[:, t * LANE:(t + 1) * LANE] = jnp.where(lane + t * LANE == local_col, 1.0, 0.0).astype(BF16)

    pl.semaphore_wait(barrier, 19)

    for n in range(SUB):
        cols = pl.ds(n * WIDE, WIDE)
        loads[n].wait()
        part = nn_dot(hot[...], emb[:, cols])
        send_d[0, :, cols] = part[0:LANE].astype(BF16)
        own[:, cols] = part[LANE:WIDE]

    def d_copy(r, k):
        src = pl.ds(pl.multiple_of(rem(line_o + k, LINE) * ROWS, ROWS), ROWS)
        return rcopy(send_d.at[r, src], recv_d.at[r, k], sd_s.at[r, k], sd_r.at[r, k], partner)

    def f_copy(r, k):
        return rcopy(send_f.at[r, k], recv_f.at[r, k], sf_s.at[r, k], sf_r.at[r, k], line_dev(k))

    def scatter_line(r):
        for k in LINE_ORDER + (0,):
            d_copy(r, k).start()
        for k in LINE_ORDER + (0,):
            d_copy(r, k).wait_recv()
            chunk = pl.ds(pl.multiple_of(rem(line + k, LINE) * ROWS, ROWS), ROWS)
            total = own[chunk, :] + recv_d[r, k].astype(F32)
            if k:
                send_f[r, k] = total.astype(BF16)
                f_copy(r, k).start()
            else:
                acc[...] = total

    def scatter_line_end(r):
        for k in (1, 3, 2):
            f_copy(r, k).wait_recv()
            acc[...] += recv_f[r, k].astype(F32)
        for t in range(TILES):
            fold32[pl.ds(t, ROWS, stride=TILES), :] = acc[:, t * LANE:(t + 1) * LANE]

    def each_plane(fn):
        def body(k, carry):
            fn(k)
            return carry
        lax.fori_loop(1, SIDE, body, 0)

    def ahead(k):
        return rem(plane + k, SIDE)

    def behind(k):
        return rem(plane + SIDE - k, SIDE)

    def p_rows(pp):
        return pl.ds(pl.multiple_of(pp * ROWS, ROWS), ROWS)

    def p_copy(r, k, slot):
        return rcopy(fold16.at[r, p_rows(ahead(k))], recv_p.at[r, slot], sp_s.at[r, k], sp_r.at[r, k], plane_dev(ahead(k)))

    def scatter_plane(r):
        each_plane(lambda k: p_copy(r, k, plane).start())

    def scatter_plane_end(r):
        each_plane(lambda k: p_copy(r, k, behind(k)).wait_recv())

        def add(k, total):
            return total + recv_p[r, behind(k)].astype(F32)
        return lax.fori_loop(1, SIDE, add, fold32[p_rows(plane), :])

    def norm_rows(values, gain):
        out = []
        for s in range(2):
            v = values[s * TILES:(s + 1) * TILES]
            v = v - jnp.sum(v, axis=(0, 1), keepdims=True) * (1.0 / D)
            var = jnp.sum(v * v, axis=(0, 1), keepdims=True) * (1.0 / D)
            out.append(v * lax.rsqrt(var + NORM_EPS) * gain)
        return jnp.concatenate(out, axis=0).astype(BF16)

    def ap_copy(r, k, slot):
        ref = ag.at[r, core, line, p_rows(slot)]
        return rcopy(ref, ref, ap_s.at[r, k], ap_r.at[r, k], plane_dev(ahead(k)))

    def al_copy(r, k, slot):
        ref = ag.at[r, core, slot]
        return rcopy(ref, ref, af_s.at[r, k], af_r.at[r, k], line_dev(k))

    def ad_copy(r, k, side, slot):
        ref = ag.at[r, side, slot]
        return rcopy(ref, ref, ad_s.at[r, k], ad_r.at[r, k], partner)

    def gather_plane(r, rows):
        ag[r, core, line, p_rows(plane), :] = rows
        each_plane(lambda k: ap_copy(r, k, plane).start())
        each_plane(lambda k: ap_copy(r, k, behind(k)).wait_recv())
        for k in LINE_ORDER:
            al_copy(r, k, line).start()
        ad_copy(r, 0, core, line).start()

    def gather_line(r):
        for k in (1, 3, 2):
            back = rem(line + LINE - k, LINE)
            al_copy(r, k, back).wait_recv()
            ad_copy(r, k, core, back).start()

    def gather_end(r):
        for k in (0, 1, 3, 2):
            ad_copy(r, k, other, rem(line_o + LINE - k, LINE)).wait_recv()

    def unfold(r, sides):
        for h in range(2):
            for q in range(LINE):
                base = (h * LINE + q) * FOLD
                unf[pl.ds(base, FOLD), :] = ag[r, sides[h], q].astype(F32)
        for t in range(TILES):
            lhs[:, t * LANE:(t + 1) * LANE] = unf[pl.ds(t, WIDE, stride=TILES), :].astype(BF16)

    scatter_line(0)

    loads[SUB].wait()
    loads[9].wait()

    def wq_rows(slot, count):
        return pl.ds(pl.multiple_of(slot * ROWS, ROWS), count * ROWS)

    wq[wq_rows(line * 2 + core, 1), :] = win[0:ROWS, :]
    wext[me_slot] = wout[0:ATT_DEV, :]

    def wd_copies():
        return (rcopy(wq.at[wq_rows(line * 2 + core, 1)], wq.at[wq_rows(line_o * 2 + core, 1)], wd_s.at[0], wd_r.at[0], partner),
                rcopy(wext.at[me_slot], wext.at[me_slot], wd_s.at[1], wd_r.at[1], partner))

    for copy in wd_copies():
        copy.start()

    def wf_copies(k, line_slot, pair_slot):
        q_ref = wq.at[wq_rows(line_slot * 2, 2)]
        e_ref = wext.at[pl.ds(pair_slot, 2)]
        return (rcopy(q_ref, q_ref, wf_s.at[0, k], wf_r.at[0, k], line_dev(k)),
                rcopy(e_ref, e_ref, wf_s.at[1, k], wf_r.at[1, k], line_dev(k)))

    my_pair = me_slot - core

    def pair_of(k):
        return my_pair + (rem(line + LINE - k, LINE) - line) * (2 + 6 * core)

    rcopy(wq.at[wq_rows(line * 2 + core, 1)], wq.at[wq_rows(line * 2 + other, 1)], wd_s.at[0], wd_r.at[0], partner).wait_recv()
    rcopy(wext.at[me_slot], wext.at[partner_slot], wd_s.at[1], wd_r.at[1], partner).wait_recv()
    for k in LINE_ORDER:
        for copy in wf_copies(k, line, my_pair):
            copy.start()

    scatter_line_end(0)
    fold16[0] = fold32[...].astype(BF16)
    scatter_plane(0)

    for t in range(TILES):
        wgu[:, t * LANE:(t + 1) * LANE] = win[QKV_DEV:QKV_DEV + WIDE, t * LANE:(t + 1) * LANE]

    def column_ids(hh):
        col = iota((1, HEAD), 1) + hh * HEAD
        src = (col * 3277) >> SIDE
        return src, col - src * QKV_DEV

    def plane_of(src):
        return jnp.where(core == 0, src >> 3, ((src >> 5) << 2) + ((src >> 1) & 3))

    def group_of(src):
        return jnp.where(core == 0, src & 7, (((src >> 3) & 3) << 1) + (src & 1))

    sel_row = iota((WIDE, HEAD), 0)
    for hh in range(10):
        src, part = column_ids(hh)
        sel[:, hh * HEAD:(hh + 1) * HEAD] = jnp.where(sel_row == group_of(src) * ROWS + part, 1.0, 0.0).astype(BF16)

    pos0 = lens_ref[me]
    pos1 = pos0 + 1

    x_val = scatter_plane_end(0)
    x_own[...] = x_val
    gather_plane(0, norm_rows(x_val, gains[0:TILES, :]))

    unf[pl.ds(0, FOLD), :] = ag[0, core, line].astype(F32)
    for s in range(2):
        for t in range(TILES):
            qlhs[s * SIDE:(s + 1) * SIDE, t * LANE:(t + 1) * LANE] = unf[pl.ds(s * TILES + t, SIDE, stride=2 * TILES), :].astype(BF16)
    for k in LINE_ORDER:
        for copy in wf_copies(k, rem(line + LINE - k, LINE), pair_of(k)):
            copy.wait_recv()
    qkv = nt_dot(qlhs[...], wq[...]).astype(BF16).astype(F32)
    qkv = jnp.where((iota((ROWS, WIDE), 1) & 31) < QKV_DEV, qkv, 0.0)
    qmsg[...] = jnp.zeros_like(qmsg)
    for s in range(2):
        for g in range(2):
            qmsg[pl.ds(s * 2 + g, SIDE, stride=SUB), :] = qkv[s * SIDE:(s + 1) * SIDE, g * LANE:(g + 1) * LANE]

    def m_rows(pp):
        return pl.ds(pl.multiple_of(pp * SUB, SUB), SUB)

    def q_copy(k, slot):
        return rcopy(qmsg.at[m_rows(ahead(k))], recv_q.at[m_rows(slot)], q_s.at[k], q_r.at[k], plane_dev(ahead(k)))

    each_plane(lambda k: q_copy(k, plane).start())
    recv_q[m_rows(plane), :] = qmsg[m_rows(plane), :]

    loads[10].wait()
    loads[11].wait()
    step_row = iota((SIDE, LANE), 0) >> 3
    angle = jnp.where(step_row == 0, pos0, pos1).astype(F32) * freq_ref[...]
    cosine = jnp.cos(angle)
    sine = jnp.sin(angle)

    gather_line(0)

    each_plane(lambda k: q_copy(k, behind(k)).wait_recv())
    for s in range(2):
        for g in range(2):
            qrows[s * SIDE:(s + 1) * SIDE, g * LANE:(g + 1) * LANE] = recv_q[pl.ds(s * 2 + g, SIDE, stride=SUB), :].astype(BF16)
    src_row = iota((SIDE, HEAD), 0)
    for hh in range(10):
        wide = nn_dot(qrows[...], sel[:, hh * HEAD:(hh + 1) * HEAD])
        keep = plane_of(column_ids(hh)[0]) == src_row
        for s in range(2):
            vec = jnp.sum(jnp.where(keep, wide[s * SIDE:(s + 1) * SIDE], 0.0), axis=0, keepdims=True)
            at = s * SUB + hh if hh < HEADS else SIDE + (hh - HEADS) * SUB + s
            qkrow[pl.ds(at, 1), :] = vec

    def rotate(vec, cos_val, sin_val):
        first, second = vec[:, :LANE], vec[:, LANE:]
        return jnp.concatenate([first * cos_val - second * sin_val, second * cos_val + first * sin_val], axis=1)

    q_rot = (rotate(qkrow[0:SIDE, :], cosine, sine) * HEAD ** -0.5).astype(BF16)
    cos_k = jnp.concatenate([cosine[0:1], cosine[SUB:9]], axis=0)
    sin_k = jnp.concatenate([sine[0:1], sine[SUB:9]], axis=0)
    k_new = rotate(qkrow[SIDE:18, :], cos_k, sin_k).astype(BF16).astype(F32)
    v_new = qkrow[24:26, :]
    for t in range(SUB):
        rows = slice(t * LANE, (t + 1) * LANE)
        time_id = iota((LANE, HEAD), 0) + t * LANE
        for buf, new in ((kbuf, k_new), (vbuf, v_new)):
            old = buf[rows, :].astype(F32)
            buf[rows, :] = jnp.where(time_id == pos0, new[0:1], jnp.where(time_id == pos1, new[1:2], old)).astype(BF16)
    stores = (pltpu.make_async_copy(kbuf, kout_hbm.at[0], ld.at[12]), pltpu.make_async_copy(vbuf, vout_hbm.at[0], ld.at[13]))
    for copy in stores:
        copy.start()
    scores = nt_dot(q_rot, kbuf[...])
    limit = jnp.where((iota((SIDE, CACHE), 0) >> 3) == 0, pos0, pos1)
    scores = jnp.where(iota((SIDE, CACHE), 1) <= limit, scores, -jnp.inf)
    probs = jnp.exp(scores - jnp.max(scores, axis=1, keepdims=True))
    probs = (probs / jnp.sum(probs, axis=1, keepdims=True)).astype(BF16)
    attn = nn_dot(probs, vbuf[...]).astype(BF16).astype(F32)
    for s in range(2):
        for g in range(2):
            afbuf[pl.ds(s * SIDE + g, SUB, stride=2), :] = attn[s * SUB:(s + 1) * SUB, g * LANE:(g + 1) * LANE]
    for zz in range(LINE):
        for s in range(2):
            amsg[zz, s * LINE:(s + 1) * LINE, :] = afbuf[s * SIDE + zz * LINE:s * SIDE + zz * LINE + LINE, :]

    def a_copy(k, slot):
        return rcopy(amsg.at[div(ahead(k), LINE)], recv_a.at[m_rows(slot)], a_s.at[k], a_r.at[k], plane_dev(ahead(k)))

    each_plane(lambda k: a_copy(k, plane).start())
    recv_a[m_rows(plane), :] = amsg[div(plane, LINE)]

    gather_end(0)
    unfold(0, (other, core))
    up_gate = nt_dot(lhs[...], wgu[...]).astype(BF16).astype(F32)
    gate, up = up_gate[:, :LANE], up_gate[:, LANE:]
    mlp[...] = (jax.nn.silu(gate) * up).astype(BF16)
    for n in range(SUB):
        cols = pl.ds(n * WIDE, WIDE)
        part = nn_dot(mlp[...], wout[pl.ds(ATT_DEV, LANE), cols])
        send_d[1, :, cols] = part[0:LANE].astype(BF16)
        own[:, cols] = part[LANE:WIDE]
    scatter_line(1)

    each_plane(lambda k: a_copy(k, behind(k)).wait_recv())
    for s in range(2):
        for g in range(LINE):
            alhs[s * SIDE:(s + 1) * SIDE, g * LANE:(g + 1) * LANE] = recv_a[pl.ds(s * LINE + g, SIDE, stride=SUB), :].astype(BF16)
    for n in range(SUB):
        cols = pl.ds(n * WIDE, WIDE)
        part = nn_dot(alhs[...], wext[:, :, cols].reshape(FOLD, WIDE))
        for s in range(2):
            for t in range(2):
                afold[pl.ds(s * TILES + n * 2 + t, SIDE, stride=2 * TILES), :] = part[s * SIDE:(s + 1) * SIDE, t * LANE:(t + 1) * LANE]
    scatter_line_end(1)
    fold32[...] += afold[...]
    fold16[1] = fold32[...].astype(BF16)
    scatter_plane(1)

    lane_q = iota((LANE, WIDE), 1)
    sub_b = iota((LANE, WIDE), 0)
    q_core = lane_q >> 7
    q_p = (lane_q >> 1) & 15
    lane_b = (q_p >> 2) * ROWS + (q_p & 3) * (SUB - 6 * q_core) + ((lane_q >> 5) & 3) * (2 + 6 * q_core) + q_core
    lane_s = lane_q & 1
    diag = iota((LANE, LANE), 0) == iota((LANE, LANE), 1)
    next_col = [jnp.sum(jnp.where(diag, next_ref[s:s + 1, :].astype(F32), 0.0), axis=1, keepdims=True) for s in range(2)]
    next_val = jnp.where(lane_s == 0, next_col[0], next_col[1])
    next_lane = jnp.sum(jnp.where(lane_b == sub_b, next_val, 0.0), axis=0, keepdims=True).astype(jnp.int32) - me * VDEV

    out_val = scatter_plane_end(1).astype(BF16).astype(F32)
    gather_plane(1, norm_rows(x_own[...] + out_val, gains[TILES:2 * TILES, :]))
    gather_line(1)
    gather_end(1)
    unfold(1, (0, 1))

    top = jnp.full((1, WIDE), -jnp.inf, F32)
    for n in range(5):
        rows = pl.ds(n * 400, 400)
        part = nt_dot(emb[rows, :], lhs[...]) * D ** -0.5
        lg[rows, :] = part
        top = jnp.maximum(top, jnp.max(part, axis=0, keepdims=True))
    exp_sum = jnp.zeros((1, WIDE), F32)
    target = jnp.zeros((1, WIDE), F32)
    for n in range(5):
        part = lg[pl.ds(n * 400, 400), :]
        exp_sum += jnp.sum(jnp.exp(part - top), axis=0, keepdims=True)
        here = iota((400, WIDE), 0) + n * 400 == next_lane
        target += jnp.sum(jnp.where(here, part, 0.0), axis=0, keepdims=True)
    local_lse = top + jnp.log(exp_sum)

    fin_s[...] = jnp.zeros_like(fin_s)
    for g in range(2):
        fin_s[0, pl.ds(g, 1), :] = local_lse[:, g * LANE:(g + 1) * LANE]
        fin_s[0, pl.ds(2 + g, 1), :] = target[:, g * LANE:(g + 1) * LANE]

    def merge(ref, count):
        high = ref[0]
        for i in range(1, count):
            high = jnp.maximum(high, ref[i])
        scale_sum = jnp.zeros((SUB, LANE), F32)
        plain_sum = jnp.zeros((SUB, LANE), F32)
        for i in range(count):
            scale_sum += jnp.exp(ref[i] - high)
            plain_sum += ref[i]
        return jnp.where(iota((SUB, LANE), 0) < 2, high + jnp.log(scale_sum), plain_sum)

    def fp_copy(k, slot):
        return rcopy(fin_s.at[0], fin_p.at[slot], fp_s.at[k], fp_r.at[k], plane_dev(ahead(k)))

    def ff_copy(k, slot):
        return rcopy(fin_s.at[1], fin_f.at[slot], ff_s.at[k], ff_r.at[k], line_dev(k))

    def fd_copy(slot):
        return rcopy(fin_s.at[2], fin_d.at[slot], fd_s.at[0], fd_r.at[0], partner)

    each_plane(lambda k: fp_copy(k, plane).start())
    fin_p[plane] = fin_s[0]
    each_plane(lambda k: fp_copy(k, behind(k)).wait_recv())
    fin_s[1] = merge(fin_p, SIDE)
    for k in LINE_ORDER:
        ff_copy(k, line).start()
    fin_f[line] = fin_s[1]
    for k in (1, 3, 2):
        ff_copy(k, rem(line + LINE - k, LINE)).wait_recv()
    fin_s[2] = merge(fin_f, LINE)
    fd_copy(core).start()
    fin_d[core] = fin_s[2]
    fd_copy(other).wait_recv()
    final = merge(fin_d, 2)
    lp_row = final[0:1, :]
    lp_lane = jnp.concatenate([final[2:3] - final[0:1], final[3:LINE] - final[1:2]], axis=1)
    for s in range(2):
        col = jnp.sum(jnp.where((lane_b == sub_b) & (lane_s == s), lp_lane, 0.0), axis=1, keepdims=True)
        logp_ref[s:s + 1, :] = jnp.sum(jnp.where(diag, col, 0.0), axis=0, keepdims=True)

    for copy in stores:
        copy.wait()
    for r in range(2):
        for k in range(LINE):
            d_copy(r, k).wait_send()
        for k in range(1, LINE):
            f_copy(r, k).wait_send()
            al_copy(r, k, line).wait_send()
        for k in range(LINE):
            ad_copy(r, k, core, line).wait_send()
        each_plane(lambda k: p_copy(r, k, plane).wait_send())
        each_plane(lambda k: ap_copy(r, k, plane).wait_send())
    for copy in wd_copies():
        copy.wait_send()
    for k in range(1, LINE):
        for copy in wf_copies(k, line, my_pair):
            copy.wait_send()
        ff_copy(k, line).wait_send()
    each_plane(lambda k: q_copy(k, plane).wait_send())
    each_plane(lambda k: a_copy(k, plane).wait_send())
    each_plane(lambda k: fp_copy(k, plane).wait_send())
    fd_copy(core).wait_send()


def solution(mesh):
    def device_fn(tok_ids, next_ids, seq_lens, embed_loc, ln_gain, w_in_loc, w_out_loc, final_gain, k_loc, v_loc):
        half_dim = HEAD // 2
        inv_freq = ROPE_BASE ** (-jnp.arange(half_dim, dtype=F32) / half_dim)
        vmem = pl.BlockSpec(memory_space=pltpu.VMEM)
        smem = pl.BlockSpec(memory_space=pltpu.SMEM)
        hbm = pl.BlockSpec(memory_space=pl.ANY)
        dma = pltpu.SemaphoreType.DMA
        scratch = [
            pltpu.VMEM((VPAD, D), BF16),
            pltpu.VMEM((276, D), BF16),
            pltpu.VMEM((WIDE, D), BF16),
            pltpu.VMEM((144, D), BF16),
            pltpu.VMEM((CACHE, HEAD), BF16),
            pltpu.VMEM((CACHE, HEAD), BF16),
            pltpu.VMEM((WIDE, D), BF16),
            pltpu.VMEM((ROWS, ATT_DEV, D), BF16),
            pltpu.VMEM((WIDE, 2560), BF16),
            pltpu.VMEM((WIDE, VPAD), BF16),
            pltpu.VMEM((2, LANE, D), BF16),
            pltpu.VMEM((LANE, D), F32),
            pltpu.VMEM((2, LINE, ROWS, D), BF16),
            pltpu.VMEM((2, LINE, ROWS, D), BF16),
            pltpu.VMEM((2, LINE, ROWS, D), BF16),
            pltpu.VMEM((ROWS, D), F32),
            pltpu.VMEM((FOLD, LANE), F32),
            pltpu.VMEM((FOLD, LANE), F32),
            pltpu.VMEM((2, FOLD, LANE), BF16),
            pltpu.VMEM((2, SIDE, ROWS, LANE), BF16),
            pltpu.VMEM((ROWS, LANE), F32),
            pltpu.VMEM((ROWS, LANE), F32),
            pltpu.VMEM((2, 2, LINE, FOLD, LANE), BF16),
            pltpu.VMEM((4096, LANE), F32),
            pltpu.VMEM((WIDE, D), BF16),
            pltpu.VMEM((ROWS, D), BF16),
            pltpu.VMEM((LANE, LANE), F32),
            pltpu.VMEM((LANE, LANE), F32),
            pltpu.VMEM((ROWS, WIDE), BF16),
            pltpu.VMEM((ROWS, HEAD), F32),
            pltpu.VMEM((ROWS, LANE), F32),
            pltpu.VMEM((LINE, SUB, LANE), F32),
            pltpu.VMEM((LANE, LANE), F32),
            pltpu.VMEM((ROWS, FOLD), BF16),
            pltpu.VMEM((WIDE, LANE), BF16),
            pltpu.VMEM((VDEV, WIDE), F32),
            pltpu.VMEM((3, SUB, LANE), F32),
            pltpu.VMEM((SIDE, SUB, LANE), F32),
            pltpu.VMEM((LINE, SUB, LANE), F32),
            pltpu.VMEM((2, SUB, LANE), F32),
            dma((14,)),
            dma((2, LINE)), dma((2, LINE)), dma((2, LINE)), dma((2, LINE)), dma((2, SIDE)), dma((2, SIDE)),
            dma((2, SIDE)), dma((2, SIDE)), dma((2, LINE)), dma((2, LINE)), dma((2, LINE)), dma((2, LINE)),
            dma((2,)), dma((2,)), dma((2, LINE)), dma((2, LINE)),
            dma((SIDE,)), dma((SIDE,)), dma((SIDE,)), dma((SIDE,)),
            dma((SIDE,)), dma((SIDE,)), dma((LINE,)), dma((LINE,)), dma((1,)), dma((1,)),
        ]
        return pl.pallas_call(
            kernel,
            out_shape=(jax.ShapeDtypeStruct(tok_ids.shape, F32),
                       jax.ShapeDtypeStruct(k_loc.shape, k_loc.dtype),
                       jax.ShapeDtypeStruct(v_loc.shape, v_loc.dtype)),
            in_specs=[vmem, vmem, smem, hbm, vmem, hbm, hbm, vmem, hbm, hbm, vmem],
            out_specs=(vmem, hbm, hbm),
            scratch_shapes=scratch,
            compiler_params=pltpu.CompilerParams(collective_id=0, has_side_effects=True, vmem_limit_bytes=60 * 2 ** 20),
        )(tok_ids, next_ids, seq_lens, embed_loc, ln_gain.reshape(1, D), w_in_loc.T, w_out_loc, final_gain.reshape(1, D),
          k_loc, v_loc, inv_freq.reshape(1, half_dim))

    cache_spec = P('tp', None, None)
    return jax.shard_map(device_fn, mesh=mesh, in_specs=(P(), P(), P(), P('tp', None), P(), P(None, 'tp'), P('tp', None), P(), cache_spec, cache_spec), out_specs=(P(), cache_spec, cache_spec), check_vma=False)
```

time: 552 us -> 91.8 us (0.17)
  waiting for transfers between devices: 322 us -> 0 us
  blocking collectives: 127 us -> 0 us
  Pallas kernels: 0 us -> 82.8 us
  other arithmetic: 23.9 us -> 0.53 us
  starting transfers between devices: 20.8 us -> 0 us
  matrix products: 18.1 us -> 0 us
  local copies, waits for them, and re-layouts: 23.1 us -> 7.56 us
  between operations: 15.8 us -> 0.64 us
    psum x2 -> x0, waiting for transfers between devices: 294 us -> none  [the longest x1 148 us: device_fn(): lax.psum(jnp.where(tok_here[:, None], emb_rows, jnp.zeros_like(emb_rows))...]
    pallas_call x0 -> x1, Pallas kernels: none -> 82.8 us  [device_fn(): pl.pallas_call(kernel, out_shape=(jax.ShapeDtypeStruct(tok_ids.shape, F32...]
    pmax x1 -> x0, blocking collectives: 63.9 us -> none  [device_fn(): row_max = lax.pmax(jnp.max(logits, axis=1), 'tp')]
    psum x1 -> x0, blocking collectives: 63.1 us -> none  [device_fn(): lax.psum(jnp.sum(jnp.exp(logits - row_max[:, None]), axis=1), 'tp')]
    all_to_all x4 -> x0, waiting for transfers between devices: 28 us -> none  [the longest x2 14.3 us: device_fn(): qkv_own = lax.all_to_all(proj_out[:, :qkv_dev], 'tp', 0, 1, tiled=True)]
    all_to_all x4 -> x0, starting transfers between devices: 20.5 us -> none  [the longest x2 11.5 us: device_fn(): qkv_own = lax.all_to_all(proj_out[:, :qkv_dev], 'tp', 0, 1, tiled=True)]
    gather x4 -> x0, local copies, waits for them, and re-layouts: 19 us -> none  [the longest x2 11.7 us: device_fn(): jnp.take(embed_loc, jnp.clip(local_ids, 0, vocab_dev - 1), axis=0)]
    dot_general x10 -> x0, matrix products: 18.1 us -> none  [the longest x2 9.51 us: device_fn(): jnp.einsum('bd,vd->bv', final_normed, embed_loc, preferred_element_type=j...]
  transfers between devices with their start and end apart: 6 -> 0, of which waited for: 6 -> 0; matrix products, arithmetic and copies ran while one was open for 3% -> 0% of each run, Pallas kernels for 0% -> 0%
where the time goes in v1:
time: 91.8 us; the launch traced here: 91.5 us
  Pallas kernels  82.8 us (90%)
  local copies, waits for them, and re-layouts  7.56 us (8%)
    pallas_call x1, Pallas kernels, device_fn(): pl.pallas_call(kernel, out_shape=(jax.ShapeDtypeStruct(tok_ids.shape, F32...  82.8 us
    unnamed x3, local copies, waits for them, and re-layouts  4.98 us

profile of v1, /device:TPU:1, one launch (start us, length us, event | category | flops | bytes accessed | tf_op | source)
XLA Modules:
  0.0 91.5 jit_solution(1290548891566750807)
XLA Ops:
  0.6 0.5 multiply_power_fusion.freq_ref
  1.2 1.3 %reshape.26.lng_ref = bf16[1,2048]{1,0:T(2,128)(2,1)} reshape(bf16[2048]{0:T(1024)(128)(2,1)} %param.14) | data formatting | bytes 8192 | tf_op jit(solution)/shard_map/reshape | solution.py:581
  2.4 1.3 %reshape.27.fing_ref = bf16[1,2048]{1,0:T(2,128)(2,1)} reshape(bf16[2048]{0:T(1024)(128)(2,1)} %param.17) | data formatting | bytes 8192 | tf_op jit(solution)/shard_map/reshape | solution.py:581
  3.7 82.8 %shard_map.121 = (f32[2,128]{1,0:T(2,128)}, bf16[1,1024,256]{2,1,0:T(8,128)(2,1)}, bf16[1,1024,256]{2,1,0:T(8,128)(2,1)}) custom-call(s32[2,128]{1,0:T(2,128)} %tok_ref.1, s32[2,128]{1,0:T(2,128)} %next_ref.1, s32[128]{0:T(128)} %lens_ref.1, bf16[2000,2048]{1,0:T(8,128)(2,1)} %emb_hbm.1, bf16[1,2048]{1,0:T(2,128)(2,1)} %reshape.26.lng_ref, ...), custom_call_target="tpu_custom_call" | custom-call | tf_op jit(solution)/shard_map/pallas_call | solution.py:572
  86.5 1.2 %copy.16 = f32[2,128]{1,0:T(2,128)} copy(f32[2,128]{1,0:T(2,128)} %get-tuple-element.6) | data formatting | bytes 2048
  87.8 1.9 %copy.17 = bf16[1,1024,256]{2,1,0:T(8,128)(2,1)} copy(bf16[1,1024,256]{2,1,0:T(8,128)(2,1)} %get-tuple-element.7) | data formatting | bytes 1048576
  89.6 1.9 %copy.18 = bf16[1,1024,256]{2,1,0:T(8,128)(2,1)} copy(bf16[1,1024,256]{2,1,0:T(8,128)(2,1)} %get-tuple-element.8) | data formatting | bytes 1048576

commit v2 on v1

--- a/solution.py
+++ b/solution.py
@@ -1,5 +1,6 @@
 import jax
 import jax.numpy as jnp
+import numpy as np
 from jax import lax
 from jax.experimental import pallas as pl
 from jax.experimental.pallas import tpu as pltpu
@@ -54,9 +55,10 @@
     return div(plane, LINE) * ROWS + rem(plane, LINE) * (SUB - 6 * core) + line * (2 + 6 * core) + core
 
 
-def kernel(tok_ref, next_ref, lens_ref, emb_hbm, lng_ref, win_hbm, wout_hbm, fing_ref, k_hbm, v_hbm, freq_ref,
-           logp_ref, kout_hbm, vout_hbm,
-           emb, win, wgu, wout, kbuf, vbuf, wq, wext, sel, hot,
+def kernel(tok_hbm, next_hbm, lens_hbm, emb_hbm, lng_hbm, win_hbm, wout_hbm, fing_hbm, k_hbm, v_hbm, freq_hbm,
+           logp_ref, kbuf, vbuf,
+           tok_ref, next_ref, lens_ref, lng_ref, fing_ref, freq_ref,
+           emb, win, wgu, wout, wq, wext, sel, hot,
            send_d, own, recv_d, send_f, recv_f, acc, fold32, afold, fold16, recv_p, x_own, gains,
            ag, unf, lhs, qlhs, qmsg, recv_q, qrows, qkrow, afbuf, amsg, recv_a, alhs, mlp, lg,
            fin_s, fin_p, fin_f, fin_d,
@@ -83,6 +85,7 @@
         return pltpu.make_async_remote_copy(src_ref=src, dst_ref=dst, send_sem=ss, recv_sem=rs, device_id=(dev,), device_id_type=MESH)
 
     def local_copies():
+        small = ((tok_hbm, tok_ref), (next_hbm, next_ref), (lng_hbm, lng_ref), (fing_hbm, fing_ref), (freq_hbm, freq_ref), (lens_hbm, lens_ref))
         out = []
         for n in range(SUB):
             cols = pl.ds(n * WIDE, WIDE)
@@ -91,10 +94,12 @@
         out.append(pltpu.make_async_copy(wout_hbm, wout, ld.at[9]))
         out.append(pltpu.make_async_copy(k_hbm.at[0], kbuf, ld.at[10]))
         out.append(pltpu.make_async_copy(v_hbm.at[0], vbuf, ld.at[11]))
+        for n, (src, dst) in enumerate(small):
+            out.append(pltpu.make_async_copy(src, dst, ld.at[12 + n]))
         return out
 
     loads = local_copies()
-    for copy in loads:
+    for copy in loads[12:] + loads[:12]:
         copy.start()
 
     wext[...] = jnp.zeros_like(wext)
@@ -110,10 +115,12 @@
 
     lax.fori_loop(1, SIDE, greet, 0)
 
+    for copy in loads[12:]:
+        copy.wait()
     emb[pl.ds(VDEV, VPAD - VDEV), :] = jnp.zeros((VPAD - VDEV, D), BF16)
     for t in range(TILES):
-        gains[pl.ds(t, 1), :] = lng_ref[:, t * LANE:(t + 1) * LANE].astype(F32)
-        gains[pl.ds(TILES + t, 1), :] = fing_ref[:, t * LANE:(t + 1) * LANE].astype(F32)
+        gains[pl.ds(t, 1), :] = lng_ref[t * LANE:(t + 1) * LANE].reshape(1, LANE).astype(F32)
+        gains[pl.ds(TILES + t, 1), :] = fing_ref[t * LANE:(t + 1) * LANE].reshape(1, LANE).astype(F32)
 
     row = iota((WIDE, LANE), 0)
     lane = iota((WIDE, LANE), 1)
@@ -127,14 +134,15 @@
     for t in range(VPAD // LANE):
         hot[:, t * LANE:(t + 1) * LANE] = jnp.where(lane + t * LANE == local_col, 1.0, 0.0).astype(BF16)
 
-    pl.semaphore_wait(barrier, 19)
-
-    for n in range(SUB):
-        cols = pl.ds(n * WIDE, WIDE)
-        loads[n].wait()
+    for n in range(LINE):
+        cols = pl.ds(n * FOLD, FOLD)
+        loads[2 * n].wait()
+        loads[2 * n + 1].wait()
         part = nn_dot(hot[...], emb[:, cols])
         send_d[0, :, cols] = part[0:LANE].astype(BF16)
         own[:, cols] = part[LANE:WIDE]
+
+    pl.semaphore_wait(barrier, 19)
 
     def d_copy(r, k):
         src = pl.ds(pl.multiple_of(rem(line_o + k, LINE) * ROWS, ROWS), ROWS)
@@ -363,9 +371,6 @@
         for buf, new in ((kbuf, k_new), (vbuf, v_new)):
             old = buf[rows, :].astype(F32)
             buf[rows, :] = jnp.where(time_id == pos0, new[0:1], jnp.where(time_id == pos1, new[1:2], old)).astype(BF16)
-    stores = (pltpu.make_async_copy(kbuf, kout_hbm.at[0], ld.at[12]), pltpu.make_async_copy(vbuf, vout_hbm.at[0], ld.at[13]))
-    for copy in stores:
-        copy.start()
     scores = nt_dot(q_rot, kbuf[...])
     limit = jnp.where((iota((SIDE, CACHE), 0) >> 3) == 0, pos0, pos1)
     scores = jnp.where(iota((SIDE, CACHE), 1) <= limit, scores, -jnp.inf)
@@ -489,8 +494,6 @@
         col = jnp.sum(jnp.where((lane_b == sub_b) & (lane_s == s), lp_lane, 0.0), axis=1, keepdims=True)
         logp_ref[s:s + 1, :] = jnp.sum(jnp.where(diag, col, 0.0), axis=0, keepdims=True)
 
-    for copy in stores:
-        copy.wait()
     for r in range(2):
         for k in range(LINE):
             d_copy(r, k).wait_send()
@@ -513,21 +516,33 @@
     fd_copy(core).wait_send()
 
 
+def finish(logp_ref, kbuf, vbuf, logp_out, kout_hbm, vout_hbm, sems):
+    copies = [pltpu.make_async_copy(kbuf, kout_hbm.at[0], sems.at[0]), pltpu.make_async_copy(vbuf, vout_hbm.at[0], sems.at[1])]
+    for copy in copies:
+        copy.start()
+    logp_out[...] = logp_ref[...]
+    for copy in copies:
+        copy.wait()
+
+
 def solution(mesh):
     def device_fn(tok_ids, next_ids, seq_lens, embed_loc, ln_gain, w_in_loc, w_out_loc, final_gain, k_loc, v_loc):
         half_dim = HEAD // 2
-        inv_freq = ROPE_BASE ** (-jnp.arange(half_dim, dtype=F32) / half_dim)
+        inv_freq = np.power(np.float32(ROPE_BASE), -np.arange(half_dim, dtype=np.float32) / half_dim).reshape(1, half_dim)
         vmem = pl.BlockSpec(memory_space=pltpu.VMEM)
-        smem = pl.BlockSpec(memory_space=pltpu.SMEM)
-        hbm = pl.BlockSpec(memory_space=pl.ANY)
+        hbm = pl.BlockSpec(memory_space=pltpu.HBM)
         dma = pltpu.SemaphoreType.DMA
         scratch = [
+            pltpu.VMEM(tok_ids.shape, jnp.int32),
+            pltpu.VMEM(next_ids.shape, jnp.int32),
+            pltpu.SMEM(seq_lens.shape, jnp.int32),
+            pltpu.VMEM((D,), BF16),
+            pltpu.VMEM((D,), BF16),
+            pltpu.VMEM((1, half_dim), F32),
             pltpu.VMEM((VPAD, D), BF16),
             pltpu.VMEM((276, D), BF16),
             pltpu.VMEM((WIDE, D), BF16),
             pltpu.VMEM((144, D), BF16),
-            pltpu.VMEM((CACHE, HEAD), BF16),
-            pltpu.VMEM((CACHE, HEAD), BF16),
             pltpu.VMEM((WIDE, D), BF16),
             pltpu.VMEM((ROWS, ATT_DEV, D), BF16),
             pltpu.VMEM((WIDE, 2560), BF16),
@@ -562,24 +577,34 @@
             pltpu.VMEM((SIDE, SUB, LANE), F32),
             pltpu.VMEM((LINE, SUB, LANE), F32),
             pltpu.VMEM((2, SUB, LANE), F32),
-            dma((14,)),
+            dma((18,)),
             dma((2, LINE)), dma((2, LINE)), dma((2, LINE)), dma((2, LINE)), dma((2, SIDE)), dma((2, SIDE)),
             dma((2, SIDE)), dma((2, SIDE)), dma((2, LINE)), dma((2, LINE)), dma((2, LINE)), dma((2, LINE)),
             dma((2,)), dma((2,)), dma((2, LINE)), dma((2, LINE)),
             dma((SIDE,)), dma((SIDE,)), dma((SIDE,)), dma((SIDE,)),
             dma((SIDE,)), dma((SIDE,)), dma((LINE,)), dma((LINE,)), dma((1,)), dma((1,)),
         ]
+        logp, k_done, v_done = pl.pallas_call(
+            kernel,
+            out_shape=(jax.ShapeDtypeStruct(tok_ids.shape, F32),
+                       jax.ShapeDtypeStruct(k_loc.shape[1:], k_loc.dtype),
+                       jax.ShapeDtypeStruct(v_loc.shape[1:], v_loc.dtype)),
+            in_specs=[hbm] * 11,
+            out_specs=(vmem, vmem, vmem),
+            scratch_shapes=scratch,
+            compiler_params=pltpu.CompilerParams(collective_id=0, has_side_effects=True, vmem_limit_bytes=48 * 2 ** 20),
+        )(*[pltpu.with_memory_space_constraint(arr, pltpu.HBM) for arr in (tok_ids, next_ids, seq_lens, embed_loc, ln_gain, w_in_loc.T, w_out_loc, final_gain,
+          k_loc, v_loc, inv_freq)])
         return pl.pallas_call(
-            kernel,
+            finish,
             out_shape=(jax.ShapeDtypeStruct(tok_ids.shape, F32),
                        jax.ShapeDtypeStruct(k_loc.shape, k_loc.dtype),
                        jax.ShapeDtypeStruct(v_loc.shape, v_loc.dtype)),
-            in_specs=[vmem, vmem, smem, hbm, vmem, hbm, hbm, vmem, hbm, hbm, vmem],
-            out_specs=(vmem, hbm, hbm),
-            scratch_shapes=scratch,
-            compiler_params=pltpu.CompilerParams(collective_id=0, has_side_effects=True, vmem_limit_bytes=60 * 2 ** 20),
-        )(tok_ids, next_ids, seq_lens, embed_loc, ln_gain.reshape(1, D), w_in_loc.T, w_out_loc, final_gain.reshape(1, D),
-          k_loc, v_loc, inv_freq.reshape(1, half_dim))
+            in_specs=[vmem, vmem, vmem],
+            out_specs=(vmem, pl.BlockSpec(memory_space=pl.ANY), pl.BlockSpec(memory_space=pl.ANY)),
+            scratch_shapes=[dma((2,))],
+            compiler_params=pltpu.CompilerParams(vmem_limit_bytes=8 * 2 ** 20),
+        )(logp, k_done, v_done)
 
     cache_spec = P('tp', None, None)
     return jax.shard_map(device_fn, mesh=mesh, in_specs=(P(), P(), P(), P('tp', None), P(), P(None, 'tp'), P('tp', None), P(), cache_spec, cache_spec), out_specs=(P(), cache_spec, cache_spec), check_vma=False)

time: 91.8 us -> 79.7 us (0.87)
  local copies, waits for them, and re-layouts: 7.56 us -> 0 us
  Pallas kernels: 82.8 us -> 78.9 us
    pallas_call x1, Pallas kernels: 82.8 us -> 77.4 us  [device_fn(): pl.pallas_call(kernel, out_shape=(jax.ShapeDtypeStruct(tok_ids.shape, F32...]
    unnamed x3 -> x0, local copies, waits for them, and re-layouts: 4.98 us -> none
    reshape x2 -> x0, local copies, waits for them, and re-layouts: 2.58 us -> none  [the longest x1 1.29 us: device_fn(): ln_gain.reshape(1, D)]
    pallas_call x0 -> x1, Pallas kernels: none -> 1.55 us  [device_fn(): pl.pallas_call(finish, out_shape=(jax.ShapeDtypeStruct(tok_ids.shape, F32...]
where the time goes in v2:
time: 79.7 us; the launch traced here: 79.6 us
  Pallas kernels  78.9 us (99%)
    pallas_call x1, Pallas kernels, device_fn(): pl.pallas_call(kernel, out_shape=(jax.ShapeDtypeStruct(tok_ids.shape, F32...  77.4 us

profile of v2, /device:TPU:1, one launch (start us, length us, event | category | flops | bytes accessed | tf_op | source)
XLA Modules:
  0.0 79.6 jit_solution(6285510629837783689)
XLA Ops:
  0.6 77.4 %shard_map.130 = (f32[2,128]{1,0:T(2,128)S(1)}, bf16[1024,256]{1,0:T(8,128)(2,1)S(1)}, bf16[1024,256]{1,0:T(8,128)(2,1)S(1)}) custom-call(s32[2,128]{1,0:T(2,128)} %tok_hbm.1, s32[2,128]{1,0:T(2,128)} %next_hbm.1, s32[128]{0:T(128)} %lens_hbm.1, bf16[2000,2048]{1,0:T(8,128)(2,1)} %emb_hbm.1, bf16[2048]{0:T(1024)(128)(2,1)} %lng_hbm.1, ...), custom_call_target="tpu_custom_call" | custom-call | tf_op jit(solution)/shard_map/pallas_call | solution.py:587
  78.0 1.5 %shard_map.131 = (f32[2,128]{1,0:T(2,128)}, bf16[1,1024,256]{2,1,0:T(8,128)(2,1)}, bf16[1,1024,256]{2,1,0:T(8,128)(2,1)}) custom-call(f32[2,128]{1,0:T(2,128)S(1)} %get-tuple-element.6.logp_ref, bf16[1024,256]{1,0:T(8,128)(2,1)S(1)} %get-tuple-element.7.kbuf, bf16[1024,256]{1,0:T(8,128)(2,1)S(1)} %get-tuple-element.8.vbuf), custom_call_target="tpu_custom_call" | custom-call | tf_op jit(solution)/shard_map/pallas_call | solution.py:598

commit v3 on v2

--- a/solution.py
+++ b/solution.py
@@ -29,6 +29,9 @@
 SUB = 8
 FOLD = 512
 LINE_ORDER = (2, 1, 3)
+ARRIVE = (1, 3, 2)
+FAR = (2, 1, 3, 0)
+NEAR = (0, 1, 3, 2)
 
 
 def rem(value, size):
@@ -59,7 +62,7 @@
            logp_ref, kbuf, vbuf,
            tok_ref, next_ref, lens_ref, lng_ref, fing_ref, freq_ref,
            emb, win, wgu, wout, wq, wext, sel, hot,
-           send_d, own, recv_d, send_f, recv_f, acc, fold32, afold, fold16, recv_p, x_own, gains,
+           send_d, own, recv_d, send_f, recv_f, total, fold32, afold, fold16, recv_p, x_own, gains,
            ag, unf, lhs, qlhs, qmsg, recv_q, qrows, qkrow, afbuf, amsg, recv_a, alhs, mlp, lg,
            fin_s, fin_p, fin_f, fin_d,
            ld, sd_s, sd_r, sf_s, sf_r, sp_s, sp_r, ap_s, ap_r, af_s, af_r, ad_s, ad_r,
@@ -70,10 +73,23 @@
     zc, yc, xc = div(me, ROWS), rem(div(me, SUB), LINE), rem(div(me, 2), LINE)
     line = xc * other + yc * core
     line_o = yc * other + xc * core
-    plane = zc * LINE + yc * other + xc * core
+    wc = yc * other + xc * core
+    plane = zc * LINE + wc
     partner = me + 1 - 2 * core
     me_slot = rem(me, ROWS)
     partner_slot = rem(partner, ROWS)
+
+    def fwd(place, k):
+        return rem(place + k, LINE)
+
+    def bck(place, k):
+        return rem(place + LINE - k, LINE)
+
+    def block(index, size):
+        return pl.ds(pl.multiple_of(index * size, size), size)
+
+    def zw_dev(zz, ww):
+        return zz * ROWS + ww * (SUB - 6 * core) + line * (2 + 6 * core) + core
 
     def line_dev(k):
         return device_of(core, rem(line + k, LINE), plane)
@@ -122,17 +138,24 @@
         gains[pl.ds(t, 1), :] = lng_ref[t * LANE:(t + 1) * LANE].reshape(1, LANE).astype(F32)
         gains[pl.ds(TILES + t, 1), :] = fing_ref[t * LANE:(t + 1) * LANE].reshape(1, LANE).astype(F32)
 
+    def sequence_of(index, own_core):
+        return ((index >> 5) & 3) * ROWS + ((index >> 1) & 3) * (SUB - 6 * own_core) + ((index >> 3) & 3) * (2 + 6 * own_core) + own_core
+
+    def half_core(index):
+        return core + (1 - (index >> 7)) * (1 - 2 * core)
+
     row = iota((WIDE, LANE), 0)
     lane = iota((WIDE, LANE), 1)
-    half = row >> 7
-    row_core = core + (1 - half) * (1 - 2 * core)
-    row_p = (row >> 1) & 15
-    row_b = (row_p >> 2) * ROWS + (row_p & 3) * (SUB - 6 * row_core) + ((row >> 5) & 3) * (2 + 6 * row_core) + row_core
+    row_b = sequence_of(row, half_core(row))
     tok_val = jnp.where((row & 1) == 0, tok_ref[0:1, :], tok_ref[1:2, :]).astype(F32)
     tok_col = jnp.sum(jnp.where(lane == row_b, tok_val, 0.0), axis=1, keepdims=True)
     local_col = tok_col.astype(jnp.int32) - me * VDEV
     for t in range(VPAD // LANE):
         hot[:, t * LANE:(t + 1) * LANE] = jnp.where(lane + t * LANE == local_col, 1.0, 0.0).astype(BF16)
+
+    def d_cols(n):
+        cols = pl.ds(n * FOLD, FOLD)
+        return rcopy(send_d.at[0, :, cols], recv_d.at[0, :, cols], sd_s.at[0, n], sd_r.at[0, n], partner)
 
     for n in range(LINE):
         cols = pl.ds(n * FOLD, FOLD)
@@ -141,35 +164,57 @@
         part = nn_dot(hot[...], emb[:, cols])
         send_d[0, :, cols] = part[0:LANE].astype(BF16)
         own[:, cols] = part[LANE:WIDE]
-
-    pl.semaphore_wait(barrier, 19)
-
-    def d_copy(r, k):
-        src = pl.ds(pl.multiple_of(rem(line_o + k, LINE) * ROWS, ROWS), ROWS)
-        return rcopy(send_d.at[r, src], recv_d.at[r, k], sd_s.at[r, k], sd_r.at[r, k], partner)
-
-    def f_copy(r, k):
-        return rcopy(send_f.at[r, k], recv_f.at[r, k], sf_s.at[r, k], sf_r.at[r, k], line_dev(k))
-
-    def scatter_line(r):
-        for k in LINE_ORDER + (0,):
-            d_copy(r, k).start()
-        for k in LINE_ORDER + (0,):
-            d_copy(r, k).wait_recv()
-            chunk = pl.ds(pl.multiple_of(rem(line + k, LINE) * ROWS, ROWS), ROWS)
-            total = own[chunk, :] + recv_d[r, k].astype(F32)
-            if k:
-                send_f[r, k] = total.astype(BF16)
-                f_copy(r, k).start()
-            else:
-                acc[...] = total
-
-    def scatter_line_end(r):
-        for k in (1, 3, 2):
-            f_copy(r, k).wait_recv()
-            acc[...] += recv_f[r, k].astype(F32)
-        for t in range(TILES):
-            fold32[pl.ds(t, ROWS, stride=TILES), :] = acc[:, t * LANE:(t + 1) * LANE]
+        if n == 2:
+            pl.semaphore_wait(barrier, 19)
+            for m in range(n):
+                d_cols(m).start()
+        if n >= 2:
+            d_cols(n).start()
+
+    def d_rows(d):
+        rows = block(fwd(zc, d), ROWS)
+        return rcopy(send_d.at[1, rows], recv_d.at[1, rows], sd_s.at[1, d], sd_r.at[1, d], partner)
+
+    def f_copy(r, k, d):
+        return rcopy(send_f.at[r, k, d], recv_f.at[r, k, d], sf_s.at[r, k, d], sf_r.at[r, k, d], line_dev(k))
+
+    def p_copy(r, d, e):
+        at = d * LINE + e
+        return rcopy(fold16.at[r, d, block(fwd(wc, e), ROWS)], recv_p.at[r, at], sp_s.at[r, at], sp_r.at[r, at], zw_dev(fwd(zc, d), fwd(wc, e)))
+
+    def scatter_send(r):
+        for d in FAR:
+            rows = block(fwd(zc, d), ROWS)
+            if r:
+                d_rows(d).wait_recv()
+            total[d] = own[rows, :] + recv_d[r, rows, :].astype(F32)
+            for k in LINE_ORDER:
+                send_f[r, k, d] = total[d, block(fwd(line, k), SUB), :].astype(BF16)
+                f_copy(r, k, d).start()
+
+    def scatter_turn(r):
+        for d in FAR:
+            part = total[d, block(line, SUB), :]
+            for k in ARRIVE:
+                f_copy(r, k, d).wait_recv()
+                part = part + recv_f[r, k, d].astype(F32)
+            for t in range(TILES):
+                fold32[d, pl.ds(t, SUB, stride=TILES), :] = part[:, t * LANE:(t + 1) * LANE]
+            if r:
+                fold32[d] += afold[block(fwd(zc, d), LANE), :]
+            fold16[r, d] = fold32[d].astype(BF16)
+            for e in FAR:
+                if d or e:
+                    p_copy(r, d, e).start()
+
+    def scatter_end(r):
+        out = fold32[0, block(wc, ROWS), :]
+        for d in NEAR:
+            for e in NEAR:
+                if d or e:
+                    p_copy(r, d, e).wait_recv()
+                    out = out + recv_p[r, d * LINE + e].astype(F32)
+        return out
 
     def each_plane(fn):
         def body(k, carry):
@@ -182,22 +227,6 @@
 
     def behind(k):
         return rem(plane + SIDE - k, SIDE)
-
-    def p_rows(pp):
-        return pl.ds(pl.multiple_of(pp * ROWS, ROWS), ROWS)
-
-    def p_copy(r, k, slot):
-        return rcopy(fold16.at[r, p_rows(ahead(k))], recv_p.at[r, slot], sp_s.at[r, k], sp_r.at[r, k], plane_dev(ahead(k)))
-
-    def scatter_plane(r):
-        each_plane(lambda k: p_copy(r, k, plane).start())
-
-    def scatter_plane_end(r):
-        each_plane(lambda k: p_copy(r, k, behind(k)).wait_recv())
-
-        def add(k, total):
-            return total + recv_p[r, behind(k)].astype(F32)
-        return lax.fori_loop(1, SIDE, add, fold32[p_rows(plane), :])
 
     def norm_rows(values, gain):
         out = []
@@ -208,45 +237,57 @@
             out.append(v * lax.rsqrt(var + NORM_EPS) * gain)
         return jnp.concatenate(out, axis=0).astype(BF16)
 
-    def ap_copy(r, k, slot):
-        ref = ag.at[r, core, line, p_rows(slot)]
-        return rcopy(ref, ref, ap_s.at[r, k], ap_r.at[r, k], plane_dev(ahead(k)))
-
-    def al_copy(r, k, slot):
-        ref = ag.at[r, core, slot]
-        return rcopy(ref, ref, af_s.at[r, k], af_r.at[r, k], line_dev(k))
-
-    def ad_copy(r, k, side, slot):
-        ref = ag.at[r, side, slot]
-        return rcopy(ref, ref, ad_s.at[r, k], ad_r.at[r, k], partner)
+    def ap_copy(r, d, e, zz, rows):
+        ref = ag.at[r, core, line, zz, rows]
+        return rcopy(ref, ref, ap_s.at[r, d * LINE + e], ap_r.at[r, d if d else LINE + e], zw_dev(fwd(zc, d), fwd(wc, e)))
+
+    def al_copy(r, k, d, place, zz):
+        ref = ag.at[r, core, place, zz]
+        return rcopy(ref, ref, af_s.at[r, k, d], af_r.at[r, k, d], line_dev(k))
+
+    def ad_copy(r, k, d, side, place, zz):
+        ref = ag.at[r, side, place, zz]
+        return rcopy(ref, ref, ad_s.at[r, k, d], ad_r.at[r, k, d], partner)
 
     def gather_plane(r, rows):
-        ag[r, core, line, p_rows(plane), :] = rows
-        each_plane(lambda k: ap_copy(r, k, plane).start())
-        each_plane(lambda k: ap_copy(r, k, behind(k)).wait_recv())
-        for k in LINE_ORDER:
-            al_copy(r, k, line).start()
-        ad_copy(r, 0, core, line).start()
+        ag[r, core, line, zc, block(wc, ROWS), :] = rows
+        for d in FAR:
+            for e in FAR:
+                if d or e:
+                    ap_copy(r, d, e, zc, block(wc, ROWS)).start()
+        for d in NEAR:
+            zz = bck(zc, d)
+            if d:
+                ap_copy(r, d, 0, zz, pl.ds(0, LANE)).wait_recv()
+            else:
+                for e in ARRIVE:
+                    ap_copy(r, 0, e, zc, block(bck(wc, e), ROWS)).wait_recv()
+            for k in LINE_ORDER:
+                al_copy(r, k, d, line, zz).start()
+            ad_copy(r, 0, d, core, line, zz).start()
 
     def gather_line(r):
-        for k in (1, 3, 2):
-            back = rem(line + LINE - k, LINE)
-            al_copy(r, k, back).wait_recv()
-            ad_copy(r, k, core, back).start()
+        for d in NEAR:
+            zz = bck(zc, d)
+            for k in ARRIVE:
+                al_copy(r, k, d, bck(line, k), zz).wait_recv()
+                ad_copy(r, k, d, core, bck(line, k), zz).start()
 
     def gather_end(r):
-        for k in (0, 1, 3, 2):
-            ad_copy(r, k, other, rem(line_o + LINE - k, LINE)).wait_recv()
-
-    def unfold(r, sides):
-        for h in range(2):
-            for q in range(LINE):
-                base = (h * LINE + q) * FOLD
-                unf[pl.ds(base, FOLD), :] = ag[r, sides[h], q].astype(F32)
+        for d in NEAR:
+            for k in (0,) + ARRIVE:
+                ad_copy(r, k, d, other, bck(line_o, k), bck(zc, d)).wait_recv()
+
+    def unfold(r, h, side):
+        for zz in range(LINE):
+            for f in range(LINE):
+                unf[pl.ds(((h * LINE + zz) * LINE + f) * LANE, LANE), :] = ag[r, side, f, zz].astype(F32)
         for t in range(TILES):
-            lhs[:, t * LANE:(t + 1) * LANE] = unf[pl.ds(t, WIDE, stride=TILES), :].astype(BF16)
-
-    scatter_line(0)
+            lhs[h * LANE:(h + 1) * LANE, t * LANE:(t + 1) * LANE] = unf[pl.ds(h * D + t, LANE, stride=TILES), :].astype(BF16)
+
+    for n in range(LINE):
+        d_cols(n).wait_recv()
+    scatter_send(0)
 
     loads[SUB].wait()
     loads[9].wait()
@@ -281,9 +322,7 @@
         for copy in wf_copies(k, line, my_pair):
             copy.start()
 
-    scatter_line_end(0)
-    fold16[0] = fold32[...].astype(BF16)
-    scatter_plane(0)
+    scatter_turn(0)
 
     for t in range(TILES):
         wgu[:, t * LANE:(t + 1) * LANE] = win[QKV_DEV:QKV_DEV + WIDE, t * LANE:(t + 1) * LANE]
@@ -307,11 +346,12 @@
     pos0 = lens_ref[me]
     pos1 = pos0 + 1
 
-    x_val = scatter_plane_end(0)
+    x_val = scatter_end(0)
     x_own[...] = x_val
     gather_plane(0, norm_rows(x_val, gains[0:TILES, :]))
 
-    unf[pl.ds(0, FOLD), :] = ag[0, core, line].astype(F32)
+    for zz in range(LINE):
+        unf[pl.ds(zz * LANE, LANE), :] = ag[0, core, line, zz].astype(F32)
     for s in range(2):
         for t in range(TILES):
             qlhs[s * SIDE:(s + 1) * SIDE, t * LANE:(t + 1) * LANE] = unf[pl.ds(s * TILES + t, SIDE, stride=2 * TILES), :].astype(BF16)
@@ -342,6 +382,19 @@
     sine = jnp.sin(angle)
 
     gather_line(0)
+    unfold(0, 1, core)
+    gather_end(0)
+    unfold(0, 0, other)
+    up_gate = nt_dot(lhs[...], wgu[...]).astype(BF16).astype(F32)
+    gate, up = up_gate[:, :LANE], up_gate[:, LANE:]
+    mlp[...] = (jax.nn.silu(gate) * up).astype(BF16)
+    for d in FAR:
+        rows = block(fwd(zc, d), ROWS)
+        rows_own = pl.ds(pl.multiple_of(LANE + fwd(zc, d) * ROWS, ROWS), ROWS)
+        part = nn_dot(jnp.concatenate([mlp[rows, :], mlp[rows_own, :]], axis=0), wout[ATT_DEV:ATT_DEV + LANE, :])
+        send_d[1, rows, :] = part[0:ROWS].astype(BF16)
+        own[rows, :] = part[ROWS:2 * ROWS]
+        d_rows(d).start()
 
     each_plane(lambda k: q_copy(k, behind(k)).wait_recv())
     for s in range(2):
@@ -390,17 +443,7 @@
     each_plane(lambda k: a_copy(k, plane).start())
     recv_a[m_rows(plane), :] = amsg[div(plane, LINE)]
 
-    gather_end(0)
-    unfold(0, (other, core))
-    up_gate = nt_dot(lhs[...], wgu[...]).astype(BF16).astype(F32)
-    gate, up = up_gate[:, :LANE], up_gate[:, LANE:]
-    mlp[...] = (jax.nn.silu(gate) * up).astype(BF16)
-    for n in range(SUB):
-        cols = pl.ds(n * WIDE, WIDE)
-        part = nn_dot(mlp[...], wout[pl.ds(ATT_DEV, LANE), cols])
-        send_d[1, :, cols] = part[0:LANE].astype(BF16)
-        own[:, cols] = part[LANE:WIDE]
-    scatter_line(1)
+    scatter_send(1)
 
     each_plane(lambda k: a_copy(k, behind(k)).wait_recv())
     for s in range(2):
@@ -412,27 +455,23 @@
         for s in range(2):
             for t in range(2):
                 afold[pl.ds(s * TILES + n * 2 + t, SIDE, stride=2 * TILES), :] = part[s * SIDE:(s + 1) * SIDE, t * LANE:(t + 1) * LANE]
-    scatter_line_end(1)
-    fold32[...] += afold[...]
-    fold16[1] = fold32[...].astype(BF16)
-    scatter_plane(1)
+    scatter_turn(1)
 
     lane_q = iota((LANE, WIDE), 1)
     sub_b = iota((LANE, WIDE), 0)
-    q_core = lane_q >> 7
-    q_p = (lane_q >> 1) & 15
-    lane_b = (q_p >> 2) * ROWS + (q_p & 3) * (SUB - 6 * q_core) + ((lane_q >> 5) & 3) * (2 + 6 * q_core) + q_core
+    lane_b = sequence_of(lane_q, half_core(lane_q))
     lane_s = lane_q & 1
     diag = iota((LANE, LANE), 0) == iota((LANE, LANE), 1)
     next_col = [jnp.sum(jnp.where(diag, next_ref[s:s + 1, :].astype(F32), 0.0), axis=1, keepdims=True) for s in range(2)]
     next_val = jnp.where(lane_s == 0, next_col[0], next_col[1])
     next_lane = jnp.sum(jnp.where(lane_b == sub_b, next_val, 0.0), axis=0, keepdims=True).astype(jnp.int32) - me * VDEV
 
-    out_val = scatter_plane_end(1).astype(BF16).astype(F32)
+    out_val = scatter_end(1).astype(BF16).astype(F32)
     gather_plane(1, norm_rows(x_own[...] + out_val, gains[TILES:2 * TILES, :]))
     gather_line(1)
+    unfold(1, 1, core)
     gather_end(1)
-    unfold(1, (0, 1))
+    unfold(1, 0, other)
 
     top = jnp.full((1, WIDE), -jnp.inf, F32)
     for n in range(5):
@@ -451,8 +490,8 @@
 
     fin_s[...] = jnp.zeros_like(fin_s)
     for g in range(2):
-        fin_s[0, pl.ds(g, 1), :] = local_lse[:, g * LANE:(g + 1) * LANE]
-        fin_s[0, pl.ds(2 + g, 1), :] = target[:, g * LANE:(g + 1) * LANE]
+        for at, vec in ((g, local_lse), (2 + g, target)):
+            fin_s[0, pl.ds(at, 1), :] = jnp.where(core == g, vec[:, LANE:], vec[:, :LANE])
 
     def merge(ref, count):
         high = ref[0]
@@ -488,22 +527,25 @@
     fin_d[core] = fin_s[2]
     fd_copy(other).wait_recv()
     final = merge(fin_d, 2)
-    lp_row = final[0:1, :]
+    lane_b = sequence_of(lane_q, lane_q >> 7)
     lp_lane = jnp.concatenate([final[2:3] - final[0:1], final[3:LINE] - final[1:2]], axis=1)
     for s in range(2):
         col = jnp.sum(jnp.where((lane_b == sub_b) & (lane_s == s), lp_lane, 0.0), axis=1, keepdims=True)
         logp_ref[s:s + 1, :] = jnp.sum(jnp.where(diag, col, 0.0), axis=0, keepdims=True)
 
+    for n in range(LINE):
+        d_cols(n).wait_send()
+        d_rows(n).wait_send()
     for r in range(2):
-        for k in range(LINE):
-            d_copy(r, k).wait_send()
-        for k in range(1, LINE):
-            f_copy(r, k).wait_send()
-            al_copy(r, k, line).wait_send()
-        for k in range(LINE):
-            ad_copy(r, k, core, line).wait_send()
-        each_plane(lambda k: p_copy(r, k, plane).wait_send())
-        each_plane(lambda k: ap_copy(r, k, plane).wait_send())
+        for d in range(LINE):
+            for k in range(LINE):
+                if k:
+                    f_copy(r, k, d).wait_send()
+                    al_copy(r, k, d, line, bck(zc, d)).wait_send()
+                ad_copy(r, k, d, core, line, bck(zc, d)).wait_send()
+                if d or k:
+                    p_copy(r, d, k).wait_send()
+                    ap_copy(r, d, k, zc, block(wc, ROWS)).wait_send()
     for copy in wd_copies():
         copy.wait_send()
     for k in range(1, LINE):
@@ -549,17 +591,17 @@
             pltpu.VMEM((WIDE, VPAD), BF16),
             pltpu.VMEM((2, LANE, D), BF16),
             pltpu.VMEM((LANE, D), F32),
-            pltpu.VMEM((2, LINE, ROWS, D), BF16),
-            pltpu.VMEM((2, LINE, ROWS, D), BF16),
-            pltpu.VMEM((2, LINE, ROWS, D), BF16),
-            pltpu.VMEM((ROWS, D), F32),
+            pltpu.VMEM((2, LANE, D), BF16),
+            pltpu.VMEM((2, LINE, LINE, SUB, D), BF16),
+            pltpu.VMEM((2, LINE, LINE, SUB, D), BF16),
+            pltpu.VMEM((LINE, ROWS, D), F32),
+            pltpu.VMEM((LINE, LANE, LANE), F32),
             pltpu.VMEM((FOLD, LANE), F32),
-            pltpu.VMEM((FOLD, LANE), F32),
-            pltpu.VMEM((2, FOLD, LANE), BF16),
+            pltpu.VMEM((2, LINE, LANE, LANE), BF16),
             pltpu.VMEM((2, SIDE, ROWS, LANE), BF16),
             pltpu.VMEM((ROWS, LANE), F32),
             pltpu.VMEM((ROWS, LANE), F32),
-            pltpu.VMEM((2, 2, LINE, FOLD, LANE), BF16),
+            pltpu.VMEM((2, 2, LINE, LINE, LANE, LANE), BF16),
             pltpu.VMEM((4096, LANE), F32),
             pltpu.VMEM((WIDE, D), BF16),
             pltpu.VMEM((ROWS, D), BF16),
@@ -578,8 +620,8 @@
             pltpu.VMEM((LINE, SUB, LANE), F32),
             pltpu.VMEM((2, SUB, LANE), F32),
             dma((18,)),
-            dma((2, LINE)), dma((2, LINE)), dma((2, LINE)), dma((2, LINE)), dma((2, SIDE)), dma((2, SIDE)),
-            dma((2, SIDE)), dma((2, SIDE)), dma((2, LINE)), dma((2, LINE)), dma((2, LINE)), dma((2, LINE)),
+            dma((2, LINE)), dma((2, LINE)), *[dma((2, LINE, LINE)) for _ in range(2)], dma((2, SIDE)), dma((2, SIDE)),
+            dma((2, SIDE)), dma((2, SUB)), *[dma((2, LINE, LINE)) for _ in range(LINE)],
             dma((2,)), dma((2,)), dma((2, LINE)), dma((2, LINE)),
             dma((SIDE,)), dma((SIDE,)), dma((SIDE,)), dma((SIDE,)),
             dma((SIDE,)), dma((SIDE,)), dma((LINE,)), dma((LINE,)), dma((1,)), dma((1,)),

time: 79.7 us -> 76.5 us (0.960)
  Pallas kernels: 78.9 us -> 75.8 us
    pallas_call x1, Pallas kernels: 77.4 us -> 74.2 us  [device_fn(): pl.pallas_call(kernel, out_shape=(jax.ShapeDtypeStruct(tok_ids.shape, F32...]
where the time goes in v3:
time: 76.5 us; the launch traced here: 76.4 us
  Pallas kernels  75.8 us (99%)
    pallas_call x1, Pallas kernels, device_fn(): pl.pallas_call(kernel, out_shape=(jax.ShapeDtypeStruct(tok_ids.shape, F32...  74.2 us
    pallas_call x1, Pallas kernels, device_fn(): pl.pallas_call(finish, out_shape=(jax.ShapeDtypeStruct(tok_ids.shape, F32...  1.55 us

profile of v3, /device:TPU:1, one launch (start us, length us, event | category | flops | bytes accessed | tf_op | source)
XLA Modules:
  0.0 76.4 jit_solution(10702095234733617698)
XLA Ops:
  0.6 74.2 %shard_map.130 = (f32[2,128]{1,0:T(2,128)S(1)}, bf16[1024,256]{1,0:T(8,128)(2,1)S(1)}, bf16[1024,256]{1,0:T(8,128)(2,1)S(1)}) custom-call(s32[2,128]{1,0:T(2,128)} %tok_hbm.1, s32[2,128]{1,0:T(2,128)} %next_hbm.1, s32[128]{0:T(128)} %lens_hbm.1, bf16[2000,2048]{1,0:T(8,128)(2,1)} %emb_hbm.1, bf16[2048]{0:T(1024)(128)(2,1)} %lng_hbm.1, ...), custom_call_target="tpu_custom_call" | custom-call | tf_op jit(solution)/shard_map/pallas_call | solution.py:629
  74.9 1.5 %shard_map.131 = (f32[2,128]{1,0:T(2,128)}, bf16[1,1024,256]{2,1,0:T(8,128)(2,1)}, bf16[1,1024,256]{2,1,0:T(8,128)(2,1)}) custom-call(f32[2,128]{1,0:T(2,128)S(1)} %get-tuple-element.6.logp_ref, bf16[1024,256]{1,0:T(8,128)(2,1)S(1)} %get-tuple-element.7.kbuf, bf16[1024,256]{1,0:T(8,128)(2,1)S(1)} %get-tuple-element.8.vbuf), custom_call_target="tpu_custom_call" | custom-call | tf_op jit(solution)/shard_map/pallas_call | solution.py:640

commit v4 on v3

v4 whole, which is shorter than its diff:
```python
import functools

import jax
import jax.numpy as jnp
import numpy as np
from jax import lax
from jax.experimental import pallas as pl
from jax.experimental.pallas import tpu as pltpu
from jax.sharding import PartitionSpec as P

ROPE_BASE = 10000.0
NORM_EPS = 1e-6
F32 = jnp.float32
BF16 = jnp.bfloat16
MESH = pl.DeviceIdType.MESH

D = 2048
VDEV = 2000
VPAD = 2048
HEADS = 8
HEAD = 256
CACHE = 1024
TILES = D // 128
QKV_DEV = 20
ATT_DEV = 16
LANE = 128
WIDE = 256
ROWS = 32
SIDE = 16
LINE = 4
SUB = 8
FOLD = 512
STEPS = 2
LINE_ORDER = (2, 1, 3)
ARRIVE = (1, 3, 2)
FAR = (2, 1, 3, 0)
NEAR = (0, 1, 3, 2)
OTHERS = pl.ds(1, 3)
THREE = pl.ds(0, 3)
FIFTEEN = pl.ds(0, 15)
FARTHER = pl.ds(LINE, 12)
PEERS = pl.ds(0, 120)


def rem(value, size):
    return lax.rem(value, jnp.int32(size))


def div(value, size):
    return lax.div(value, jnp.int32(size))


def iota(shape, dim):
    return lax.broadcasted_iota(jnp.int32, shape, dim)


def nt_dot(left, right):
    return lax.dot_general(left, right, (((1,), (1,)), ((), ())), preferred_element_type=F32)


def nn_dot(left, right):
    return lax.dot_general(left, right, (((1,), (0,)), ((), ())), preferred_element_type=F32)


def device_of(core, line, plane):
    return div(plane, LINE) * ROWS + rem(plane, LINE) * (SUB - 6 * core) + line * (2 + 6 * core) + core


def kernel(tok_hbm, next_hbm, lens_hbm, emb_hbm, lng_hbm, win_hbm, wout_hbm, fing_hbm, k_hbm, v_hbm, freq_hbm,
           logp_ref, kbuf, vbuf,
           tok_ref, next_ref, lens_ref, lng_ref, fing_ref, freq_ref,
           emb, win, wgu, wout, wq, wext, sel, hot,
           send_d, own, recv_d, send_f, recv_f, total, fold32, afold, fold16, recv_p, x_own, gains,
           ag, unf, lhs, qlhs, qmsg, recv_q, qrows, qkrow, afbuf, amsg, recv_a, alhs, mlp,
           fin_s, fin_p, fin_f, fin_d,
           ld, sd_s, sd_r, sf_s, sf_r, sp_s, sp_r, ap_s, ap_r, af_s, af_r, ad_s, ad_r,
           wd_s, wd_r, wf_s, wf_r, q_s, q_r, a_s, a_r, fp_s, fp_r, ff_s, ff_r, fd_s, fd_r):
    me = lax.axis_index('tp')
    core = rem(me, 2)
    other = 1 - core
    zc, yc, xc = div(me, ROWS), rem(div(me, SUB), LINE), rem(div(me, 2), LINE)
    line = xc * other + yc * core
    line_o = yc * other + xc * core
    wc = yc * other + xc * core
    plane = zc * LINE + wc
    partner = me + 1 - 2 * core
    me_slot = rem(me, ROWS)
    partner_slot = rem(partner, ROWS)

    def fwd(place, k):
        return rem(place + k, LINE)

    def bck(place, k):
        return rem(place + LINE - k, LINE)

    def block(index, size):
        return pl.ds(pl.multiple_of(index * size, size), size)

    def zw_dev(zz, ww):
        return zz * ROWS + ww * (SUB - 6 * core) + line * (2 + 6 * core) + core

    def line_dev(k):
        return device_of(core, rem(line + k, LINE), plane)

    def plane_dev(pp):
        return device_of(core, line, pp)

    def rcopy(src, dst, ss, rs, dev):
        return pltpu.make_async_remote_copy(src_ref=src, dst_ref=dst, send_sem=ss, recv_sem=rs, device_id=(dev,), device_id_type=MESH)

    def take(ref, sem):
        pltpu.make_async_copy(ref, ref, sem).wait()

    def local_copies():
        small = ((tok_hbm, tok_ref), (next_hbm, next_ref), (lng_hbm, lng_ref), (fing_hbm, fing_ref), (freq_hbm, freq_ref), (lens_hbm, lens_ref))
        out = []
        for n in range(LINE):
            cols = pl.ds(n * FOLD, FOLD)
            out.append(pltpu.make_async_copy(emb_hbm.at[:, cols], emb.at[pl.ds(0, VDEV), cols], ld.at[n]))
        out.append(pltpu.make_async_copy(win_hbm, win, ld.at[4]))
        out.append(pltpu.make_async_copy(wout_hbm, wout, ld.at[5]))
        out.append(pltpu.make_async_copy(k_hbm.at[0], kbuf, ld.at[6]))
        out.append(pltpu.make_async_copy(v_hbm.at[0], vbuf, ld.at[7]))
        for n, (src, dst) in enumerate(small):
            out.append(pltpu.make_async_copy(src, dst, ld.at[8 + n]))
        return out

    loads = local_copies()
    for copy in loads[8:] + loads[:8]:
        copy.start()

    wext[...] = jnp.zeros_like(wext)
    wq[...] = jnp.zeros_like(wq)

    barrier = pltpu.get_barrier_semaphore()
    pl.semaphore_signal(barrier, inc=1, device_id=(partner,), device_id_type=MESH)
    for k in range(1, LINE):
        pl.semaphore_signal(barrier, inc=1, device_id=(line_dev(k),), device_id_type=MESH)

    def greet(k, carry):
        pl.semaphore_signal(barrier, inc=1, device_id=(plane_dev(rem(plane + k, SIDE)),), device_id_type=MESH)
        return carry

    lax.fori_loop(1, SIDE, greet, 0)

    for copy in loads[8:]:
        copy.wait()
    emb[pl.ds(VDEV, VPAD - VDEV), :] = jnp.zeros((VPAD - VDEV, D), BF16)
    for t in range(TILES):
        gains[pl.ds(t, 1), :] = lng_ref[t * LANE:(t + 1) * LANE].reshape(1, LANE).astype(F32)
        gains[pl.ds(TILES + t, 1), :] = fing_ref[t * LANE:(t + 1) * LANE].reshape(1, LANE).astype(F32)

    def sequence_of(index, own_core):
        return ((index >> 5) & 3) * ROWS + ((index >> 1) & 3) * (SUB - 6 * own_core) + ((index >> 3) & 3) * (2 + 6 * own_core) + own_core

    def half_core(index):
        return core + (1 - (index >> 7)) * (1 - 2 * core)

    row = iota((WIDE, LANE), 0)
    lane = iota((WIDE, LANE), 1)
    row_b = sequence_of(row, half_core(row))
    tok_val = jnp.where((row & 1) == 0, tok_ref[0:1, :], tok_ref[1:2, :]).astype(F32)
    tok_col = jnp.sum(jnp.where(lane == row_b, tok_val, 0.0), axis=1, keepdims=True)
    local_col = tok_col.astype(jnp.int32) - me * VDEV
    for t in range(VPAD // LANE):
        hot[:, t * LANE:(t + 1) * LANE] = jnp.where(lane + t * LANE == local_col, 1.0, 0.0).astype(BF16)

    def d_cols(n):
        cols = pl.ds(n * FOLD, FOLD)
        return rcopy(send_d.at[0, :, cols], recv_d.at[0, :, cols], sd_s.at[0], sd_r.at[0], partner)

    for n in range(LINE):
        cols = pl.ds(n * FOLD, FOLD)
        loads[n].wait()
        part = nn_dot(hot[...], emb[:, cols])
        send_d[0, :, cols] = part[0:LANE].astype(BF16)
        own[:, cols] = part[LANE:WIDE]
        if n == 2:
            pl.semaphore_wait(barrier, 19)
            for m in range(n):
                d_cols(m).start()
        if n >= 2:
            d_cols(n).start()

    def d_rows(d):
        rows = block(fwd(zc, d), ROWS)
        return rcopy(send_d.at[1, rows], recv_d.at[1, rows], sd_s.at[1], sd_r.at[1 + d], partner)

    def f_copy(r, k, d):
        return rcopy(send_f.at[r, k, d], recv_f.at[r, k, d], sf_s.at[r], sf_r.at[r, d], line_dev(k))

    def p_copy(r, d, e):
        at = d * LINE + e
        return rcopy(fold16.at[r, d, block(fwd(wc, e), ROWS)], recv_p.at[r, at], sp_s.at[r, min(d, 1)], sp_r.at[r, min(d, 1)], zw_dev(fwd(zc, d), fwd(wc, e)))

    def scatter_send(r):
        for d in FAR:
            rows = block(fwd(zc, d), ROWS)
            if r:
                d_rows(d).wait_recv()
            total[d] = own[rows, :] + recv_d[r, rows, :].astype(F32)
            for k in LINE_ORDER:
                send_f[r, k, d] = total[d, block(fwd(line, k), SUB), :].astype(BF16)
                f_copy(r, k, d).start()

    def scatter_turn(r):
        for d in FAR:
            part = total[d, block(line, SUB), :]
            take(recv_f.at[r, OTHERS, d], sf_r.at[r, d])
            for k in ARRIVE:
                part = part + recv_f[r, k, d].astype(F32)
            for t in range(TILES):
                fold32[d, pl.ds(t, SUB, stride=TILES), :] = part[:, t * LANE:(t + 1) * LANE]
            if r:
                fold32[d] += afold[block(fwd(zc, d), LANE), :]
            fold16[r, d] = fold32[d].astype(BF16)
            for e in FAR:
                if d or e:
                    p_copy(r, d, e).start()

    def scatter_end(r):
        out = fold32[0, block(wc, ROWS), :]
        take(recv_p.at[r, OTHERS], sp_r.at[r, 0])
        take(recv_p.at[r, FARTHER], sp_r.at[r, 1])
        for at in range(1, SIDE):
            out = out + recv_p[r, at].astype(F32)
        return out

    def each_plane(fn):
        def body(k, carry):
            fn(k)
            return carry
        lax.fori_loop(1, SIDE, body, 0)

    def ahead(k):
        return rem(plane + k, SIDE)

    def behind(k):
        return rem(plane + SIDE - k, SIDE)

    def norm_rows(values, gain):
        out = []
        for s in range(STEPS):
            v = values[s * TILES:(s + 1) * TILES]
            v = v - jnp.sum(v, axis=(0, 1), keepdims=True) * (1.0 / D)
            var = jnp.sum(v * v, axis=(0, 1), keepdims=True) * (1.0 / D)
            out.append(v * lax.rsqrt(var + NORM_EPS) * gain)
        return jnp.concatenate(out, axis=0).astype(BF16)

    def ap_copy(r, d, e, zz, rows):
        ref = ag.at[r, core, line, zz, rows]
        return rcopy(ref, ref, ap_s.at[r, min(d, 1)], ap_r.at[r, d], zw_dev(fwd(zc, d), fwd(wc, e)))

    def al_copy(r, k, d, place, zz):
        ref = ag.at[r, core, place, zz]
        return rcopy(ref, ref, af_s.at[r], af_r.at[r, d], line_dev(k))

    def ad_copy(r, side, place, zz):
        ref = ag.at[r, side, place, zz]
        return rcopy(ref, ref, ad_s.at[r], ad_r.at[r], partner)

    def gather_plane(r, rows):
        ag[r, core, line, zc, block(wc, ROWS), :] = rows
        for d in FAR:
            for e in FAR:
                if d or e:
                    ap_copy(r, d, e, zc, block(wc, ROWS)).start()
        for d in NEAR:
            zz = bck(zc, d)
            take(ag.at[r, core, line, zz, pl.ds(0, LANE if d else 3 * ROWS)], ap_r.at[r, d])
            for k in LINE_ORDER:
                al_copy(r, k, d, line, zz).start()
            ad_copy(r, core, line, zz).start()

    def gather_line(r):
        for d in NEAR:
            zz = bck(zc, d)
            take(ag.at[r, core, THREE, zz], af_r.at[r, d])
            for k in ARRIVE:
                ad_copy(r, core, bck(line, k), zz).start()

    def gather_end(r):
        take(ag.at[r, other], ad_r.at[r])

    def unfold(r, h, side):
        for zz in range(LINE):
            for f in range(LINE):
                unf[pl.ds(((h * LINE + zz) * LINE + f) * LANE, LANE), :] = ag[r, side, f, zz].astype(F32)
        for t in range(TILES):
            lhs[h * LANE:(h + 1) * LANE, t * LANE:(t + 1) * LANE] = unf[pl.ds(h * D + t, LANE, stride=TILES), :].astype(BF16)

    take(recv_d.at[0], sd_r.at[0])
    scatter_send(0)

    loads[4].wait()
    loads[5].wait()

    def wq_rows(slot, count):
        return pl.ds(pl.multiple_of(slot * ROWS, ROWS), count * ROWS)

    wq[wq_rows(line * 2 + core, 1), :] = win[0:ROWS, :]
    wext[me_slot] = wout[0:ATT_DEV, :]
    my_pair = me_slot - core

    def wd_copies():
        return (rcopy(wq.at[wq_rows(line * 2 + core, 1)], wq.at[wq_rows(line_o * 2 + core, 1)], wd_s.at[0], wd_r.at[0], partner),
                rcopy(wext.at[me_slot], wext.at[me_slot], wd_s.at[0], wd_r.at[0], partner))

    def wq_copy(k, g):
        ref = wq.at[pl.ds(pl.multiple_of((line * 2 + g) * ROWS, ROWS), 24)]
        return rcopy(ref, ref, wf_s.at[0], wf_r.at[0], line_dev(k))

    def wext_copy(k):
        ref = wext.at[pl.ds(my_pair, 2)]
        return rcopy(ref, ref, wf_s.at[1], wf_r.at[1], line_dev(k))

    for copy in wd_copies():
        copy.start()
    take(wext.at[THREE], wd_r.at[0])
    for k in LINE_ORDER:
        for g in range(STEPS):
            wq_copy(k, g).start()

    scatter_turn(0)

    for t in range(TILES):
        wgu[:, t * LANE:(t + 1) * LANE] = win[QKV_DEV:QKV_DEV + WIDE, t * LANE:(t + 1) * LANE]

    def column_ids(hh):
        col = iota((1, HEAD), 1) + hh * HEAD
        src = (col * 3277) >> SIDE
        return src, col - src * QKV_DEV

    def plane_of(src):
        return jnp.where(core == 0, src >> 3, ((src >> 5) << 2) + ((src >> 1) & 3))

    def group_of(src):
        return jnp.where(core == 0, src & 7, (((src >> 3) & 3) << 1) + (src & 1))

    sel_row = iota((WIDE, HEAD), 0)
    for hh in range(10):
        src, part = column_ids(hh)
        sel[:, hh * HEAD:(hh + 1) * HEAD] = jnp.where(sel_row == group_of(src) * ROWS + part, 1.0, 0.0).astype(BF16)

    pos0 = lens_ref[me]
    pos1 = pos0 + 1

    x_val = scatter_end(0)
    x_own[...] = x_val
    gather_plane(0, norm_rows(x_val, gains[0:TILES, :]))

    for zz in range(LINE):
        unf[pl.ds(zz * LANE, LANE), :] = ag[0, core, line, zz].astype(F32)
    for s in range(STEPS):
        for t in range(TILES):
            qlhs[s * SIDE:(s + 1) * SIDE, t * LANE:(t + 1) * LANE] = unf[pl.ds(s * TILES + t, SIDE, stride=2 * TILES), :].astype(BF16)
    take(wext.at[pl.ds(0, 9)], wf_r.at[0])
    qkv = nt_dot(qlhs[...], wq[...]).astype(BF16).astype(F32)
    qkv = jnp.where((iota((ROWS, WIDE), 1) & 31) < QKV_DEV, qkv, 0.0)
    qmsg[...] = jnp.zeros_like(qmsg)
    for s in range(STEPS):
        for g in range(STEPS):
            qmsg[pl.ds(s * 2 + g, SIDE, stride=SUB), :] = qkv[s * SIDE:(s + 1) * SIDE, g * LANE:(g + 1) * LANE]

    def m_rows(pp):
        return pl.ds(pl.multiple_of(pp * SUB, SUB), SUB)

    def q_copy(k, slot):
        return rcopy(qmsg.at[m_rows(ahead(k))], recv_q.at[m_rows(slot)], q_s.at[0], q_r.at[0], plane_dev(ahead(k)))

    each_plane(lambda k: q_copy(k, plane).start())
    recv_q[m_rows(plane), :] = qmsg[m_rows(plane), :]

    loads[6].wait()
    loads[7].wait()
    step_row = iota((SIDE, LANE), 0) >> 3
    angle = jnp.where(step_row == 0, pos0, pos1).astype(F32) * freq_ref[...]
    cosine = jnp.cos(angle)
    sine = jnp.sin(angle)

    gather_line(0)
    for k in LINE_ORDER:
        wext_copy(k).start()

    take(recv_q.at[PEERS], q_r.at[0])
    for s in range(STEPS):
        for g in range(STEPS):
            qrows[s * SIDE:(s + 1) * SIDE, g * LANE:(g + 1) * LANE] = recv_q[pl.ds(s * 2 + g, SIDE, stride=SUB), :].astype(BF16)
    src_row = iota((SIDE, HEAD), 0)
    for hh in range(10):
        wide = nn_dot(qrows[...], sel[:, hh * HEAD:(hh + 1) * HEAD])
        keep = plane_of(column_ids(hh)[0]) == src_row
        for s in range(STEPS):
            vec = jnp.sum(jnp.where(keep, wide[s * SIDE:(s + 1) * SIDE], 0.0), axis=0, keepdims=True)
            at = s * SUB + hh if hh < HEADS else SIDE + (hh - HEADS) * SUB + s
            qkrow[pl.ds(at, 1), :] = vec

    def rotate(vec, cos_val, sin_val):
        first, second = vec[:, :LANE], vec[:, LANE:]
        return jnp.concatenate([first * cos_val - second * sin_val, second * cos_val + first * sin_val], axis=1)

    q_rot = (rotate(qkrow[0:SIDE, :], cosine, sine) * HEAD ** -0.5).astype(BF16)
    cos_k = jnp.concatenate([cosine[0:1], cosine[SUB:9]], axis=0)
    sin_k = jnp.concatenate([sine[0:1], sine[SUB:9]], axis=0)
    k_new = rotate(qkrow[SIDE:18, :], cos_k, sin_k).astype(BF16).astype(F32)
    v_new = qkrow[24:26, :]
    for t in range(SUB):
        rows = slice(t * LANE, (t + 1) * LANE)
        time_id = iota((LANE, HEAD), 0) + t * LANE
        for buf, new in ((kbuf, k_new), (vbuf, v_new)):
            old = buf[rows, :].astype(F32)
            buf[rows, :] = jnp.where(time_id == pos0, new[0:1], jnp.where(time_id == pos1, new[1:2], old)).astype(BF16)
    scores = nt_dot(q_rot, kbuf[...])
    limit = jnp.where((iota((SIDE, CACHE), 0) >> 3) == 0, pos0, pos1)
    scores = jnp.where(iota((SIDE, CACHE), 1) <= limit, scores, -jnp.inf)
    probs = jnp.exp(scores - jnp.max(scores, axis=1, keepdims=True))
    probs = (probs / jnp.sum(probs, axis=1, keepdims=True)).astype(BF16)
    attn = nn_dot(probs, vbuf[...]).astype(BF16).astype(F32)
    for s in range(STEPS):
        for g in range(STEPS):
            afbuf[pl.ds(s * SIDE + g, SUB, stride=2), :] = attn[s * SUB:(s + 1) * SUB, g * LANE:(g + 1) * LANE]
    for zz in range(LINE):
        for s in range(STEPS):
            amsg[zz, s * LINE:(s + 1) * LINE, :] = afbuf[s * SIDE + zz * LINE:s * SIDE + zz * LINE + LINE, :]

    def a_copy(k, slot):
        return rcopy(amsg.at[div(ahead(k), LINE)], recv_a.at[m_rows(slot)], a_s.at[0], a_r.at[0], plane_dev(ahead(k)))

    each_plane(lambda k: a_copy(k, plane).start())
    recv_a[m_rows(plane), :] = amsg[div(plane, LINE)]

    unfold(0, 1, core)
    gather_end(0)
    unfold(0, 0, other)
    up_gate = nt_dot(lhs[...], wgu[...]).astype(BF16).astype(F32)
    gate, up = up_gate[:, :LANE], up_gate[:, LANE:]
    mlp[...] = (jax.nn.silu(gate) * up).astype(BF16)
    for d in FAR:
        rows = block(fwd(zc, d), ROWS)
        rows_own = pl.ds(pl.multiple_of(LANE + fwd(zc, d) * ROWS, ROWS), ROWS)
        part = nn_dot(jnp.concatenate([mlp[rows, :], mlp[rows_own, :]], axis=0), wout[ATT_DEV:ATT_DEV + LANE, :])
        send_d[1, rows, :] = part[0:ROWS].astype(BF16)
        own[rows, :] = part[ROWS:2 * ROWS]
        d_rows(d).start()

    scatter_send(1)

    take(wext.at[pl.ds(0, 6)], wf_r.at[1])
    take(recv_a.at[PEERS], a_r.at[0])
    for s in range(STEPS):
        for g in range(LINE):
            alhs[s * SIDE:(s + 1) * SIDE, g * LANE:(g + 1) * LANE] = recv_a[pl.ds(s * LINE + g, SIDE, stride=SUB), :].astype(BF16)
    for n in range(SUB):
        cols = pl.ds(n * WIDE, WIDE)
        part = nn_dot(alhs[...], wext[:, :, cols].reshape(FOLD, WIDE))
        for s in range(STEPS):
            for t in range(STEPS):
                afold[pl.ds(s * TILES + n * 2 + t, SIDE, stride=2 * TILES), :] = part[s * SIDE:(s + 1) * SIDE, t * LANE:(t + 1) * LANE]
    scatter_turn(1)

    lane_q = iota((LANE, WIDE), 1)
    sub_b = iota((LANE, WIDE), 0)
    lane_b = sequence_of(lane_q, half_core(lane_q))
    lane_s = lane_q & 1
    diag = iota((LANE, LANE), 0) == iota((LANE, LANE), 1)
    next_col = [jnp.sum(jnp.where(diag, next_ref[s:s + 1, :].astype(F32), 0.0), axis=1, keepdims=True) for s in range(STEPS)]
    next_val = jnp.where(lane_s == 0, next_col[0], next_col[1])
    next_lane = jnp.sum(jnp.where(lane_b == sub_b, next_val, 0.0), axis=0, keepdims=True).astype(jnp.int32) - me * VDEV

    out_val = scatter_end(1).astype(BF16).astype(F32)
    gather_plane(1, norm_rows(x_own[...] + out_val, gains[TILES:2 * TILES, :]))
    gather_line(1)
    unfold(1, 1, core)
    gather_end(1)
    unfold(1, 0, other)

    tops, sums = [], []
    target = jnp.zeros((1, WIDE), F32)
    for n in range(5):
        part = nt_dot(emb[pl.ds(n * 400, 400), :], lhs[...]) * D ** -0.5
        tops.append(jnp.max(part, axis=0, keepdims=True))
        sums.append(jnp.sum(jnp.exp(part - tops[n]), axis=0, keepdims=True))
        here = iota((400, WIDE), 0) + n * 400 == next_lane
        target += jnp.sum(jnp.where(here, part, 0.0), axis=0, keepdims=True)
    top = functools.reduce(jnp.maximum, tops)
    local_lse = top + jnp.log(sum(jnp.exp(t - top) * e for t, e in zip(tops, sums)))

    fin_s[...] = jnp.zeros_like(fin_s)
    for g in range(STEPS):
        for at, vec in ((g, local_lse), (2 + g, target)):
            fin_s[0, pl.ds(at, 1), :] = jnp.where(core == g, vec[:, LANE:], vec[:, :LANE])

    def merge(parts):
        high = functools.reduce(jnp.maximum, parts)
        scale_sum = sum(jnp.exp(part - high) for part in parts)
        return jnp.where(iota((SUB, LANE), 0) < 2, high + jnp.log(scale_sum), sum(parts))

    def fp_copy(k):
        return rcopy(fin_s.at[1], fin_p.at[plane], fp_s.at[0], fp_r.at[0], plane_dev(ahead(k)))

    def ff_copy(k):
        return rcopy(fin_s.at[2], fin_f.at[line], ff_s.at[0], ff_r.at[0], line_dev(k))

    down = rcopy(fin_s.at[0], fin_d.at[0], fd_s.at[0], fd_r.at[0], partner)
    back = rcopy(fin_s.at[3], fin_d.at[1], fd_s.at[0], fd_r.at[0], partner)

    @pl.when(core == 0)
    def _():
        down.start()
        back.wait_recv()
        down.wait_send()

    @pl.when(core == 1)
    def _():
        down.wait_recv()
        fin_s[1] = merge([fin_d[0], fin_s[0]])
        each_plane(lambda k: fp_copy(k).start())
        fin_p[plane] = fin_s[1]
        take(fin_p.at[FIFTEEN], fp_r.at[0])
        fin_s[2] = merge([fin_p[i] for i in range(SIDE)])
        for k in LINE_ORDER:
            ff_copy(k).start()
        fin_f[line] = fin_s[2]
        take(fin_f.at[THREE], ff_r.at[0])
        fin_s[3] = merge([fin_f[i] for i in range(LINE)])
        back.start()
        fin_d[1] = fin_s[3]
        take(fin_p.at[FIFTEEN], fp_s.at[0])
        take(fin_f.at[THREE], ff_s.at[0])
        back.wait_send()

    final = fin_d[1]
    lane_b = sequence_of(lane_q, lane_q >> 7)
    lp_lane = jnp.concatenate([final[2:3] - final[0:1], final[3:LINE] - final[1:2]], axis=1)
    for s in range(STEPS):
        col = jnp.sum(jnp.where((lane_b == sub_b) & (lane_s == s), lp_lane, 0.0), axis=1, keepdims=True)
        logp_ref[s:s + 1, :] = jnp.sum(jnp.where(diag, col, 0.0), axis=0, keepdims=True)

    for r in range(STEPS):
        take(send_d.at[r], sd_s.at[r])
        take(send_f.at[r, OTHERS], sf_s.at[r])
        take(recv_p.at[r, OTHERS], sp_s.at[r, 0])
        take(recv_p.at[r, FARTHER], sp_s.at[r, 1])
        take(recv_p.at[r, OTHERS], ap_s.at[r, 0])
        take(recv_p.at[r, FARTHER], ap_s.at[r, 1])
        take(ag.at[r, core, THREE], af_s.at[r])
        take(ag.at[r, core], ad_s.at[r])
    take(wext.at[THREE], wd_s.at[0])
    take(wext.at[pl.ds(0, 9)], wf_s.at[0])
    take(wext.at[pl.ds(0, 6)], wf_s.at[1])
    take(recv_q.at[PEERS], q_s.at[0])
    take(recv_a.at[PEERS], a_s.at[0])


def finish(logp_ref, kbuf, vbuf, logp_out, kout_hbm, vout_hbm, sems):
    copies = [pltpu.make_async_copy(kbuf, kout_hbm.at[0], sems.at[0]), pltpu.make_async_copy(vbuf, vout_hbm.at[0], sems.at[1])]
    for copy in copies:
        copy.start()
    logp_out[...] = logp_ref[...]
    for copy in copies:
        copy.wait()


def solution(mesh):
    def device_fn(tok_ids, next_ids, seq_lens, embed_loc, ln_gain, w_in_loc, w_out_loc, final_gain, k_loc, v_loc):
        half_dim = HEAD // 2
        inv_freq = np.power(np.float32(ROPE_BASE), -np.arange(half_dim, dtype=np.float32) / half_dim).reshape(1, half_dim)
        vmem = pl.BlockSpec(memory_space=pltpu.VMEM)
        hbm = pl.BlockSpec(memory_space=pltpu.HBM)
        dma = pltpu.SemaphoreType.DMA
        scratch = [
            pltpu.VMEM(tok_ids.shape, jnp.int32),
            pltpu.VMEM(next_ids.shape, jnp.int32),
            pltpu.SMEM(seq_lens.shape, jnp.int32),
            pltpu.VMEM((D,), BF16),
            pltpu.VMEM((D,), BF16),
            pltpu.VMEM((1, half_dim), F32),
            pltpu.VMEM((VPAD, D), BF16),
            pltpu.VMEM((276, D), BF16),
            pltpu.VMEM((WIDE, D), BF16),
            pltpu.VMEM((144, D), BF16),
            pltpu.VMEM((WIDE, D), BF16),
            pltpu.VMEM((ROWS, ATT_DEV, D), BF16),
            pltpu.VMEM((WIDE, 2560), BF16),
            pltpu.VMEM((WIDE, VPAD), BF16),
            pltpu.VMEM((STEPS, LANE, D), BF16),
            pltpu.VMEM((LANE, D), F32),
            pltpu.VMEM((STEPS, LANE, D), BF16),
            pltpu.VMEM((STEPS, LINE, LINE, SUB, D), BF16),
            pltpu.VMEM((STEPS, LINE, LINE, SUB, D), BF16),
            pltpu.VMEM((LINE, ROWS, D), F32),
            pltpu.VMEM((LINE, LANE, LANE), F32),
            pltpu.VMEM((FOLD, LANE), F32),
            pltpu.VMEM((STEPS, LINE, LANE, LANE), BF16),
            pltpu.VMEM((STEPS, SIDE, ROWS, LANE), BF16),
            pltpu.VMEM((ROWS, LANE), F32),
            pltpu.VMEM((ROWS, LANE), F32),
            pltpu.VMEM((STEPS, 2, LINE, LINE, LANE, LANE), BF16),
            pltpu.VMEM((4096, LANE), F32),
            pltpu.VMEM((WIDE, D), BF16),
            pltpu.VMEM((ROWS, D), BF16),
            pltpu.VMEM((LANE, LANE), F32),
            pltpu.VMEM((LANE, LANE), F32),
            pltpu.VMEM((ROWS, WIDE), BF16),
            pltpu.VMEM((ROWS, HEAD), F32),
            pltpu.VMEM((ROWS, LANE), F32),
            pltpu.VMEM((LINE, SUB, LANE), F32),
            pltpu.VMEM((LANE, LANE), F32),
            pltpu.VMEM((ROWS, FOLD), BF16),
            pltpu.VMEM((WIDE, LANE), BF16),
            pltpu.VMEM((LINE, SUB, LANE), F32),
            pltpu.VMEM((SIDE, SUB, LANE), F32),
            pltpu.VMEM((LINE, SUB, LANE), F32),
            pltpu.VMEM((STEPS, SUB, LANE), F32),
            dma((14,)),
            dma((STEPS,)), dma((5,)), dma((STEPS,)), dma((STEPS, LINE)), dma((STEPS, STEPS)), dma((STEPS, STEPS)),
            dma((STEPS, STEPS)), dma((STEPS, LINE)), dma((STEPS,)), dma((STEPS, LINE)), dma((STEPS,)), dma((STEPS,)),
            dma((1,)), dma((1,)), dma((STEPS,)), dma((STEPS,)),
            *[dma((1,)) for _ in range(10)],
        ]
        logp, k_done, v_done = pl.pallas_call(
            kernel,
            out_shape=(jax.ShapeDtypeStruct(tok_ids.shape, F32),
                       jax.ShapeDtypeStruct(k_loc.shape[1:], k_loc.dtype),
                       jax.ShapeDtypeStruct(v_loc.shape[1:], v_loc.dtype)),
            in_specs=[hbm] * 11,
            out_specs=(vmem, vmem, vmem),
            scratch_shapes=scratch,
            compiler_params=pltpu.CompilerParams(collective_id=0, has_side_effects=True, vmem_limit_bytes=48 * 2 ** 20),
        )(*[pltpu.with_memory_space_constraint(arr, pltpu.HBM) for arr in (tok_ids, next_ids, seq_lens, embed_loc, ln_gain, w_in_loc.T, w_out_loc, final_gain,
          k_loc, v_loc, inv_freq)])
        return pl.pallas_call(
            finish,
            out_shape=(jax.ShapeDtypeStruct(tok_ids.shape, F32),
                       jax.ShapeDtypeStruct(k_loc.shape, k_loc.dtype),
                       jax.ShapeDtypeStruct(v_loc.shape, v_loc.dtype)),
            in_specs=[vmem, vmem, vmem],
            out_specs=(vmem, pl.BlockSpec(memory_space=pl.ANY), pl.BlockSpec(memory_space=pl.ANY)),
            scratch_shapes=[dma((STEPS,))],
            compiler_params=pltpu.CompilerParams(vmem_limit_bytes=8 * 2 ** 20),
        )(logp, k_done, v_done)

    cache_spec = P('tp', None, None)
    return jax.shard_map(device_fn, mesh=mesh, in_specs=(P(), P(), P(), P('tp', None), P(), P(None, 'tp'), P('tp', None), P(), cache_spec, cache_spec), out_specs=(P(), cache_spec, cache_spec), check_vma=False)
```

time: 76.5 us -> 69.4 us (0.907)
  Pallas kernels: 75.8 us -> 68.6 us
    pallas_call x1, Pallas kernels: 74.2 us -> 67.1 us  [device_fn(): pl.pallas_call(kernel, out_shape=(jax.ShapeDtypeStruct(tok_ids.shape, F32...]
where the time goes in v4:
time: 69.4 us; the launch traced here: 69.3 us
  Pallas kernels  68.6 us (99%)
    pallas_call x1, Pallas kernels, device_fn(): pl.pallas_call(kernel, out_shape=(jax.ShapeDtypeStruct(tok_ids.shape, F32...  67.1 us
    pallas_call x1, Pallas kernels, device_fn(): pl.pallas_call(finish, out_shape=(jax.ShapeDtypeStruct(tok_ids.shape, F32...  1.55 us

profile of v4, /device:TPU:1, one launch (start us, length us, event | category | flops | bytes accessed | tf_op | source)
XLA Modules:
  0.0 69.3 jit_solution(3475728421703591341)
XLA Ops:
  0.6 67.1 %shard_map.130 = (f32[2,128]{1,0:T(2,128)S(1)}, bf16[1024,256]{1,0:T(8,128)(2,1)S(1)}, bf16[1024,256]{1,0:T(8,128)(2,1)S(1)}) custom-call(s32[2,128]{1,0:T(2,128)} %tok_hbm.1, s32[2,128]{1,0:T(2,128)} %next_hbm.1, s32[128]{0:T(128)} %lens_hbm.1, bf16[2000,2048]{1,0:T(8,128)(2,1)} %emb_hbm.1, bf16[2048]{0:T(1024)(128)(2,1)} %lng_hbm.1, ...), custom_call_target="tpu_custom_call" | custom-call | tf_op jit(solution)/shard_map/pallas_call | solution.py:621
  67.7 1.5 %shard_map.131 = (f32[2,128]{1,0:T(2,128)}, bf16[1,1024,256]{2,1,0:T(8,128)(2,1)}, bf16[1,1024,256]{2,1,0:T(8,128)(2,1)}) custom-call(f32[2,128]{1,0:T(2,128)S(1)} %get-tuple-element.6.logp_ref, bf16[1024,256]{1,0:T(8,128)(2,1)S(1)} %get-tuple-element.7.kbuf, bf16[1024,256]{1,0:T(8,128)(2,1)S(1)} %get-tuple-element.8.vbuf), custom_call_target="tpu_custom_call" | custom-call | tf_op jit(solution)/shard_map/pallas_call | solution.py:632
